TPU v7x, 32 devices: a whole 2x2x4 slice. The times are simulated.
32 devices in a mesh: rows: 4 (over y, core), cols: 8 (over z, x), hub: 1.
Axes of the slice: x: 2, y: 2, z: 4, core: 2. Of those that a mesh axis runs over, the one named last changes fastest.
Arguments:
- light_bits: int32 [96, 3072], P('rows', 'cols'), may hold values from -2147483648 to 2147483647, as said below
- hub_bits: int32 [4, 3072], P('hub', 'cols'), may hold values from -2147483648 to 2147483647, as said below
- hub_ids: int32 [128], replicated, may hold values from 0 to 3071, as said below
Outputs:
- clustering: float32 [3072], P(('rows', 'cols'))
Inputs may be any that keep to these rules, and one draw needn't show every extreme that they name: Every word holds 32 bits; the matrix of light_bits is symmetric with a zero diagonal. `hub_bits`: every word holds 32 bits. `hub_ids`: 128 distinct vertex numbers.
All inputs are finite; a program needn't handle non-finite values.
Results may differ from a plain program's by a relative error of at most 0.0003.
Values sent between devices are 32-bit elements; how exact they have to be, the bound alone decides.
A program may use at most 128 MiB of HBM per device.

v0:
```python
import functools

import jax
import jax.numpy as jnp
from jax import lax
from jax.experimental import pallas as pl
from jax.experimental.pallas import tpu as pltpu
from jax.sharding import PartitionSpec as P

LANES = 128
MESH = pl.DeviceIdType.MESH


def spread(row, value, other=0.0):
    masks = jnp.left_shift(jnp.int32(1), lax.broadcasted_iota(jnp.int32, (32, row.shape[1]), 0))
    return jnp.where((jnp.broadcast_to(row, masks.shape) & masks) != 0, value, other)


def kernel(
    R, C, G,
    light_hbm, hub_hbm, ids_ref, out_ref,
    rowbuf, colbuf, hubbuf, keep, hubcol, abuf, bbuf, acc, wsum, outbox, inbox, flags,
    local_sem, row_send, row_recv, col_send, col_recv, hub_send, hub_recv, msg_send, msg_recv,
):
    r, c, g = lax.axis_index("rows"), lax.axis_index("cols"), lax.axis_index("hub")
    _, bw, bc = rowbuf.shape
    hw = hubbuf.shape[1]
    pc = bc // G
    q = C // R
    rows = 32 * bw
    wq = bw // q
    nh = 32 * hw * G
    per = rows // C
    me = g * C + c

    own = [
        pltpu.make_async_copy(light_hbm, rowbuf.at[c], local_sem.at[0]),
        pltpu.make_async_copy(hub_hbm, hubbuf.at[me], local_sem.at[1]),
        pltpu.make_async_copy(light_hbm, colbuf.at[r], local_sem.at[2]),
    ]
    for copy in own:
        copy.start()

    def group_peer(d):
        slot = lax.rem(me + d, G * C)
        return slot, (r, lax.rem(slot, C), slot // C)

    def col_peer(d):
        slot = lax.rem(r + d, R)
        return slot, (slot, c, g)

    barrier = pltpu.get_barrier_semaphore()
    for d in range(1, G * C):
        pl.semaphore_signal(barrier, inc=1, device_id=group_peer(d)[1], device_id_type=MESH)
    for d in range(1, R):
        pl.semaphore_signal(barrier, inc=1, device_id=col_peer(d)[1], device_id_type=MESH)

    for copy in own:
        copy.wait()
    pl.semaphore_wait(barrier, G * C - 1 + R - 1)

    half = C // 2
    home = c // q == r
    inner = jnp.logical_and(4 * c >= C, 4 * c < 3 * C)

    def hub_copy(dj, d):
        return pltpu.make_async_remote_copy(
            src_ref=hubbuf.at[me], dst_ref=hubbuf.at[me], send_sem=hub_send.at[dj * C + d],
            recv_sem=hub_recv.at[me], device_id_type=MESH,
            device_id=(r, lax.rem(c + C - d, C), lax.rem(g + G - dj, G)))

    hub_offsets = [(dj, d) for d in range(C - 1, -1, -1) for dj in range(G) if dj or d]

    def hub_moves(act):
        for dj, d in hub_offsets:
            if d <= half:
                act(dj, d)
            else:
                pl.when(home)(functools.partial(act, dj, d))

    hub_moves(lambda dj, d: hub_copy(dj, d).start())
    sends = []
    for d in range(half, 0, -1):
        sends.append(pltpu.make_async_remote_copy(
            src_ref=rowbuf.at[c], dst_ref=rowbuf.at[c], send_sem=row_send.at[d], recv_sem=row_recv.at[c],
            device_id=(r, lax.rem(c + C - d, C), g), device_id_type=MESH))
    for d in range(1, R):
        sends.append(pltpu.make_async_remote_copy(
            src_ref=colbuf.at[r], dst_ref=colbuf.at[r], send_sem=col_send.at[d], recv_sem=col_recv.at[r],
            device_id=col_peer(d)[1], device_id_type=MESH))
    pl.when(jnp.logical_not(inner))(sends[0].start)
    for copy in sends[1:]:
        copy.start()

    for h in range(nh // LANES):
        hubcol[h * LANES:(h + 1) * LANES, :] = jnp.transpose(
            jnp.broadcast_to(ids_ref[h:h + 1, :], (LANES, LANES)))

    def hub_hits(base):
        return hubcol[...] == base + lax.broadcasted_iota(jnp.int32, (nh, LANES), 1)

    def light_lanes(t, carry):
        hit = jnp.max(jnp.where(hub_hits(t * LANES), 1, 0), axis=0, keepdims=True)
        keep[pl.ds(t, 1), :] = hit - 1
        return carry

    tiles = bc // LANES
    lax.fori_loop(0, C * tiles, light_lanes, 0)

    def keep_of(block):
        return jnp.concatenate([keep[pl.ds(block * tiles + t, 1), :] for t in range(tiles)], axis=1)

    part = pl.ds(pl.multiple_of(g * pc, LANES), pc)
    first = (g == 0).astype(jnp.float32)
    ones = jnp.full((bc, LANES), 1.0, jnp.float32)

    def load(d):
        ck = lax.rem(c + d, C)
        rk = ck // q
        base = d * bc + (nh if d else 0)
        weight = 1.0 if d == 0 else 2.0
        word0 = lax.rem(ck, q) * wq
        for w in range(wq):
            at = base + 32 * w
            bbuf[at:at + 32, :pc] = spread(colbuf[rk, pl.ds(word0 + w, 1), part], weight).astype(jnp.bfloat16)
        if d == 0:
            bbuf[base:base + bc, pc:] = (ones * first).astype(jnp.bfloat16)
        mask = keep_of(ck)
        for w in range(bw):
            abuf[32 * w:32 * w + 32, base:base + bc] = spread(
                rowbuf[ck, w:w + 1, :] & mask, 1.0).astype(jnp.bfloat16)
        for j in range(G):
            for w in range(hw):
                at = rows + 32 * (j * hw + w)
                abuf[at:at + 32, base:base + bc] = spread(
                    hubbuf[j * C + ck, w:w + 1, :] & mask, 1.0).astype(jnp.bfloat16)

    for d in range(1, R):
        slot = col_peer(d)[0]
        pltpu.make_async_copy(colbuf.at[slot], colbuf.at[slot], col_recv.at[slot]).wait()
    load(0)

    def hub_wait(slot):
        pltpu.make_async_copy(hubbuf.at[slot], hubbuf.at[slot], hub_recv.at[slot]).wait()

    for dj, d in hub_offsets:
        ck = lax.rem(c + d, C)
        wait = functools.partial(hub_wait, lax.rem(g + dj, G) * C + ck)
        if d <= half:
            wait()
        else:
            pl.when(ck // q == r)(wait)

    once = first * (c == 0).astype(jnp.float32)
    for j in range(G):
        for w in range(hw):
            at = bc + 32 * (j * hw + w)
            bbuf[at:at + 32, :pc] = spread(hubbuf[j * C + c, w:w + 1, part], 2.0).astype(jnp.bfloat16)
    bbuf[bc:bc + nh, pc:] = jnp.broadcast_to(once, (nh, LANES)).astype(jnp.bfloat16)
    abuf[rows:, bc:bc + nh] = jnp.zeros((nh, nh), jnp.bfloat16)
    for j in range(G):
        for k in range(q):
            bits = jnp.concatenate(
                [spread(hubbuf[j * C + r * q + k, w:w + 1, :], 1.0) for w in range(hw)], axis=0)
            lanes = slice(bc + 32 * hw * j, bc + 32 * hw * (j + 1))
            abuf[k * bc:(k + 1) * bc, lanes] = jnp.transpose(bits).astype(jnp.bfloat16)
    done = bc + nh
    acc[...] = jnp.dot(abuf[:, :done], bbuf[:done, :], preferred_element_type=jnp.float32)

    def settle(to, d):
        hits = hub_hits(r * rows + to * per)
        light = 1.0 - jnp.sum(jnp.where(hits, 1.0, 0.0), axis=0, keepdims=True)
        start = pl.multiple_of(to * per, 8)
        own_sum = jnp.transpose(acc[pl.ds(start, LANES), pc:])[:1, :]
        outbox[d, 1:2, :] = light * own_sum + jnp.sum(
            jnp.where(hits, acc[rows:, pc:], 0.0), axis=0, keepdims=True)
        flags[d] = light

    for d in range(G * C):
        settle(lax.rem(group_peer(d)[0], C), d)

    def meet(d):
        ck = lax.rem(c + d, C)
        pltpu.make_async_copy(rowbuf.at[ck], rowbuf.at[ck], row_recv.at[ck]).wait()
        load(d)

    def add(begin, end):
        acc[:, :pc] += jnp.dot(abuf[:, begin:end], bbuf[begin:end, :pc], preferred_element_type=jnp.float32)

    for d in range(1, half):
        meet(d)
        if d % 2 == 0 or d == half - 1:
            add(done, (d + 1) * bc + nh)
            done = (d + 1) * bc + nh

    @pl.when(inner)
    def _():
        meet(half)
        add(done, (half + 1) * bc + nh)

    mask = jnp.concatenate(
        [keep[pl.ds(c * tiles + g * (pc // LANES) + t, 1), :] for t in range(pc // LANES)], axis=1)

    def close(row, at):
        hit = spread(row & mask, acc[at:at + 32, :pc])
        wsum[at:at + 32, :] = functools.reduce(
            jnp.add, [hit[:, t * LANES:(t + 1) * LANES] for t in range(pc // LANES)])

    for w in range(bw):
        close(rowbuf[c, w:w + 1, part], 32 * w)
    for j in range(G):
        for w in range(hw):
            close(hubbuf[j * C + c, w:w + 1, part], rows + 32 * (j * hw + w))

    hub_tri = jnp.sum(wsum[rows:, :], axis=1, keepdims=True)

    def partial(to, d):
        hits = hub_hits(r * rows + to * per)
        start = pl.multiple_of(to * per, 8)
        own_sum = jnp.sum(jnp.transpose(wsum[pl.ds(start, LANES), :]), axis=0, keepdims=True)
        return flags[d] * own_sum + jnp.sum(jnp.where(hits, hub_tri, 0.0), axis=0, keepdims=True)

    posts = []
    for d in sorted(range(1, G * C), key=lambda d: abs(2 * d - G * C)):
        slot, peer = group_peer(d)
        outbox[d, 0:1, :] = partial(lax.rem(slot, C), d)
        post = pltpu.make_async_remote_copy(
            src_ref=outbox.at[d], dst_ref=inbox.at[me], send_sem=msg_send.at[d], recv_sem=msg_recv.at[me],
            device_id=peer, device_id_type=MESH)
        post.start()
        posts.append(post)

    tri = partial(c, 0)
    deg = outbox[0, 1:2, :]
    for d in range(1, G * C):
        slot, _ = group_peer(d)
        pltpu.make_async_copy(inbox.at[slot], inbox.at[slot], msg_recv.at[slot]).wait()
        tri = tri + inbox[slot, 0:1, :]
        deg = deg + inbox[slot, 1:2, :]
    out_ref[...] = (0.5 * tri / (1.0 + deg))[:, :per]
    hub_moves(lambda dj, d: hub_copy(dj, d).wait_send())
    pl.when(jnp.logical_not(inner))(sends[0].wait_send)
    for copy in sends[1:] + posts:
        copy.wait_send()


def body(light_bits, hub_bits, hub_ids):
    R, C, G = lax.axis_size("rows"), lax.axis_size("cols"), lax.axis_size("hub")
    bw, bc = light_bits.shape
    hw = hub_bits.shape[0]
    nh = hub_ids.shape[0]
    rows, pc = 32 * bw, bc // G
    per = rows // C
    depth = (C // 2 + 1) * bc + nh
    dma = pltpu.SemaphoreType.DMA
    out = pl.pallas_call(
        functools.partial(kernel, R, C, G),
        out_shape=jax.ShapeDtypeStruct((1, per), jnp.float32),
        in_specs=[
            pl.BlockSpec(memory_space=pl.ANY),
            pl.BlockSpec(memory_space=pl.ANY),
            pl.BlockSpec(memory_space=pltpu.VMEM),
        ],
        out_specs=pl.BlockSpec(memory_space=pltpu.VMEM),
        scratch_shapes=[
            pltpu.VMEM((C, bw, bc), jnp.int32),
            pltpu.VMEM((R, bw, bc), jnp.int32),
            pltpu.VMEM((G * C, hw, bc), jnp.int32),
            pltpu.VMEM((C * bc // LANES, LANES), jnp.int32),
            pltpu.VMEM((nh, LANES), jnp.int32),
            pltpu.VMEM((rows + nh, depth), jnp.bfloat16),
            pltpu.VMEM((depth, pc + LANES), jnp.bfloat16),
            pltpu.VMEM((rows + nh, pc + LANES), jnp.float32),
            pltpu.VMEM((rows + nh, LANES), jnp.float32),
            pltpu.VMEM((G * C, 2, LANES), jnp.float32),
            pltpu.VMEM((G * C, 2, LANES), jnp.float32),
            pltpu.VMEM((G * C, 1, LANES), jnp.float32),
            dma((3,)), dma((C,)), dma((C,)), dma((R,)), dma((R,)),
            dma((G * C,)), dma((G * C,)), dma((G * C,)), dma((G * C,)),
        ],
        compiler_params=pltpu.CompilerParams(
            collective_id=0, has_side_effects=True, vmem_limit_bytes=56 * 1024 * 1024),
    )(light_bits, hub_bits, hub_ids.reshape(nh // LANES, LANES))
    return out.reshape(per)


def solution(mesh):
    return jax.shard_map(
        body,
        mesh=mesh,
        in_specs=(P("rows", "cols"), P("hub", "cols"), P()),
        out_specs=P(("rows", "cols")),
        check_vma=False,
    )
```

profile of v0, /device:TPU:0, one launch (start us, length us, event | category | flops | bytes accessed | tf_op | source)
XLA Modules:
  0.0 22.0 jit_solution(1432050032220660626)
XLA Ops:
  0.0 20.9 %shard_map.37 = f32[1,96]{1,0:T(1,128)} custom-call(s32[24,384]{1,0:T(8,128)} %light_hbm.1, s32[4,384]{1,0:T(4,128)} %hub_hbm.1, s32[1,128]{1,0:T(1,128)} %bitcast.2), custom_call_target="tpu_custom_call" | custom-call | tf_op jit(solution)/shard_map/pallas_call | solution.py:256
  20.9 0.0 copy-start
  20.9 0.6 %copy-done = f32[1,96]{1,0:T(1,128)S(1)} copy-done((f32[1,96]{1,0:T(1,128)S(1)}, f32[1,96]{1,0:T(1,128)}, u32[]{:S(2)}) %copy-start) | copy-done | bytes 408
  21.5 0.5 %copy.5 = f32[96]{0:T(128)} copy(f32[96]{0:T(128)S(1)} %bitcast.3) | data formatting | bytes 768
Async XLA Ops:
  20.9 0.6 %copy-start = (f32[1,96]{1,0:T(1,128)S(1)}, f32[1,96]{1,0:T(1,128)}, u32[]{:S(2)}) copy-start(f32[1,96]{1,0:T(1,128)} %shard_map.37) | copy-start | bytes 1156
where the time goes:
time: 22.2 us; the launch traced here: 22 us
  Pallas kernels  20.9 us (94%)
  local copies, waits for them, and re-layouts  1.1 us (5%)
    pallas_call x1, Pallas kernels, body(): pl.pallas_call(functools.partial(kernel, R, C, G), out_shape=jax.ShapeDty...  20.9 us
    unnamed x3, local copies, waits for them, and re-layouts  1.1 us

commit v1 on v0

--- a/solution.py
+++ b/solution.py
@@ -1,4 +1,5 @@
 import functools
+import math
 
 import jax
 import jax.numpy as jnp
@@ -18,8 +19,8 @@
 
 def kernel(
     R, C, G,
-    light_hbm, hub_hbm, ids_ref, out_ref,
-    rowbuf, colbuf, hubbuf, keep, hubcol, abuf, bbuf, acc, wsum, outbox, inbox, flags,
+    light_hbm, hub_hbm, ids_hbm, out_ref,
+    ids_ref, rowbuf, colbuf, hubbuf, keep, hubcol, abuf, bbuf, acc, wsum, outbox, inbox, flags,
     local_sem, row_send, row_recv, col_send, col_recv, hub_send, hub_recv, msg_send, msg_recv,
 ):
     r, c, g = lax.axis_index("rows"), lax.axis_index("cols"), lax.axis_index("hub")
@@ -37,6 +38,7 @@
         pltpu.make_async_copy(light_hbm, rowbuf.at[c], local_sem.at[0]),
         pltpu.make_async_copy(hub_hbm, hubbuf.at[me], local_sem.at[1]),
         pltpu.make_async_copy(light_hbm, colbuf.at[r], local_sem.at[2]),
+        pltpu.make_async_copy(ids_hbm, ids_ref, local_sem.at[3]),
     ]
     for copy in own:
         copy.start()
@@ -253,34 +255,36 @@
     per = rows // C
     depth = (C // 2 + 1) * bc + nh
     dma = pltpu.SemaphoreType.DMA
+    hbm = pl.BlockSpec(memory_space=pltpu.HBM)
+    buffers = [
+        ((nh // LANES, LANES), jnp.int32),
+        ((C, bw, bc), jnp.int32),
+        ((R, bw, bc), jnp.int32),
+        ((G * C, hw, bc), jnp.int32),
+        ((C * bc // LANES, LANES), jnp.int32),
+        ((nh, LANES), jnp.int32),
+        ((rows + nh, depth), jnp.bfloat16),
+        ((depth, pc + LANES), jnp.bfloat16),
+        ((rows + nh, pc + LANES), jnp.float32),
+        ((rows + nh, LANES), jnp.float32),
+        ((G * C, 2, LANES), jnp.float32),
+        ((G * C, 2, LANES), jnp.float32),
+        ((G * C, 1, LANES), jnp.float32),
+    ]
+    held = sum(math.prod(shape) * jnp.dtype(dtype).itemsize for shape, dtype in buffers)
     out = pl.pallas_call(
         functools.partial(kernel, R, C, G),
         out_shape=jax.ShapeDtypeStruct((1, per), jnp.float32),
-        in_specs=[
-            pl.BlockSpec(memory_space=pl.ANY),
-            pl.BlockSpec(memory_space=pl.ANY),
-            pl.BlockSpec(memory_space=pltpu.VMEM),
-        ],
+        in_specs=[hbm, hbm, hbm],
         out_specs=pl.BlockSpec(memory_space=pltpu.VMEM),
-        scratch_shapes=[
-            pltpu.VMEM((C, bw, bc), jnp.int32),
-            pltpu.VMEM((R, bw, bc), jnp.int32),
-            pltpu.VMEM((G * C, hw, bc), jnp.int32),
-            pltpu.VMEM((C * bc // LANES, LANES), jnp.int32),
-            pltpu.VMEM((nh, LANES), jnp.int32),
-            pltpu.VMEM((rows + nh, depth), jnp.bfloat16),
-            pltpu.VMEM((depth, pc + LANES), jnp.bfloat16),
-            pltpu.VMEM((rows + nh, pc + LANES), jnp.float32),
-            pltpu.VMEM((rows + nh, LANES), jnp.float32),
-            pltpu.VMEM((G * C, 2, LANES), jnp.float32),
-            pltpu.VMEM((G * C, 2, LANES), jnp.float32),
-            pltpu.VMEM((G * C, 1, LANES), jnp.float32),
-            dma((3,)), dma((C,)), dma((C,)), dma((R,)), dma((R,)),
+        scratch_shapes=[pltpu.VMEM(shape, dtype) for shape, dtype in buffers] + [
+            dma((4,)), dma((C,)), dma((C,)), dma((R,)), dma((R,)),
             dma((G * C,)), dma((G * C,)), dma((G * C,)), dma((G * C,)),
         ],
         compiler_params=pltpu.CompilerParams(
-            collective_id=0, has_side_effects=True, vmem_limit_bytes=56 * 1024 * 1024),
-    )(light_bits, hub_bits, hub_ids.reshape(nh // LANES, LANES))
+            collective_id=0, has_side_effects=True, vmem_limit_bytes=held + 12 * 1024 * 1024),
+    )(*(pltpu.with_memory_space_constraint(x, pltpu.HBM)
+        for x in (light_bits, hub_bits, hub_ids.reshape(nh // LANES, LANES))))
     return out.reshape(per)
 
 

time: 22.2 us -> 20.5 us (0.923)
  Pallas kernels: 20.9 us -> 19.8 us
  local copies, waits for them, and re-layouts: 1.1 us -> 0.51 us
    pallas_call x1, Pallas kernels: 20.9 us -> 19.8 us  [body(): pl.pallas_call(functools.partial(kernel, R, C, G), out_shape=jax.ShapeDty...]
    unnamed x3 -> x1, local copies, waits for them, and re-layouts: 1.1 us -> 0.51 us
where the time goes in v1:
time: 20.5 us; the launch traced here: 20.3 us
  Pallas kernels  19.8 us (97%)
  local copies, waits for them, and re-layouts  0.51 us (2%)
    pallas_call x1, Pallas kernels, body(): pl.pallas_call(functools.partial(kernel, R, C, G), out_shape=jax.ShapeDty...  19.8 us
    unnamed x1, local copies, waits for them, and re-layouts  0.51 us

profile of v1, /device:TPU:0, one launch (start us, length us, event | category | flops | bytes accessed | tf_op | source)
XLA Modules:
  0.0 20.3 jit_solution(7872202978342666375)
XLA Ops:
  0.0 19.8 %shard_map.37 = f32[1,96]{1,0:T(1,128)S(1)} custom-call(s32[24,384]{1,0:T(8,128)} %light_hbm.1, s32[4,384]{1,0:T(4,128)} %hub_hbm.1, s32[1,128]{1,0:T(1,128)} %bitcast.3), custom_call_target="tpu_custom_call" | custom-call | tf_op jit(solution)/shard_map/pallas_call | solution.py:275
  19.8 0.5 %copy.5 = f32[96]{0:T(128)} copy(f32[96]{0:T(128)S(1)} %bitcast.2) | data formatting | bytes 768

commit v2 on v1

v2 whole, which is shorter than its diff:
```python
import functools
import math

import jax
import jax.numpy as jnp
from jax import lax
from jax.experimental import pallas as pl
from jax.experimental.pallas import tpu as pltpu
from jax.sharding import PartitionSpec as P

LANES = 128
MESH = pl.DeviceIdType.MESH


def spread(row, value, other=0.0):
    masks = jnp.left_shift(jnp.int32(1), lax.broadcasted_iota(jnp.int32, (32, row.shape[1]), 0))
    return jnp.where((jnp.broadcast_to(row, masks.shape) & masks) != 0, value, other)


def piece(bw, wq, q):
    starts = [x * wq // 8 * 8 for x in range(q)]
    size = max(-(-(x + 1) * wq // 8) * 8 - starts[x] for x in range(q))
    if max(starts) + size > bw:
        return 0, bw
    return 8, size


def kernel(
    R, C, G,
    light_hbm, hub_hbm, ids_hbm, out_ref,
    ids_ref, rowbuf, colbuf, hubbuf, keep, hubcol, abuf, bbuf, home, degs, wsum, outbox, inbox, flags,
    local_sem, row_send, row_recv, col_send, col_recv, hub_send, hub_recv, msg_send, msg_recv,
):
    r, c, g = lax.axis_index("rows"), lax.axis_index("cols"), lax.axis_index("hub")
    _, bw, bc = rowbuf.shape
    hw = hubbuf.shape[1]
    pc = bc // G
    q = C // R
    z, x = c // q, c % q
    rows = 32 * bw
    wq = bw // q
    ng = 32 * hw
    nh = ng * G
    per = rows // C
    me = g * C + c
    unit, size = piece(bw, wq, q)

    def begin(x):
        return x * wq // unit * unit if unit else 0 * x

    own = [
        pltpu.make_async_copy(light_hbm, rowbuf.at[c], local_sem.at[0]),
        pltpu.make_async_copy(hub_hbm, hubbuf.at[me], local_sem.at[1]),
        pltpu.make_async_copy(ids_hbm, ids_ref, local_sem.at[2]),
    ]
    for copy in own:
        copy.start()

    def at(plane, dx, dg=0):
        return (r, plane * q + (x + dx) % q, (g + dg) % G)

    barrier = pltpu.get_barrier_semaphore()

    def greet(device):
        pl.semaphore_signal(barrier, inc=1, device_id=device, device_id_type=MESH)

    for dz in range(R):
        @pl.when(z + dz < R)
        def _():
            for dx in range(q):
                for dg in range(G):
                    if dz or dx or dg:
                        greet(at(z + dz, dx, dg))
    for dr in range(1, R):
        @pl.when((r + dr) % R >= z)
        def _():
            for dx in range(q):
                greet(((r + dr) % R, z * q + dx, g))

    def row_copy(dz, dx):
        return pltpu.make_async_remote_copy(
            src_ref=rowbuf.at[c], dst_ref=rowbuf.at[c], send_sem=row_send.at[dz, dx], recv_sem=row_recv.at[c],
            device_id=at(z - dz, dx), device_id_type=MESH)

    def hub_copy(dz, dx, dg):
        return pltpu.make_async_remote_copy(
            src_ref=hubbuf.at[me], dst_ref=hubbuf.at[me], send_sem=hub_send.at[dz, dx, dg],
            recv_sem=hub_recv.at[me], device_id=at(z - dz, dx, dg), device_id_type=MESH)

    def col_copy(dr, tx):
        return pltpu.make_async_remote_copy(
            src_ref=rowbuf.at[c, pl.ds(begin(tx), size), :], dst_ref=colbuf.at[r, x],
            send_sem=col_send.at[dr, tx], recv_sem=col_recv.at[r, x],
            device_id=((r + dr) % R, z * q + tx, g), device_id_type=MESH)

    def moves(act):
        for dz in range(R - 1, -1, -1):
            @pl.when(z >= dz)
            def _():
                for dx in range(q):
                    for dg in range(G):
                        if dz or dx or dg:
                            act(hub_copy(dz, dx, dg))
                if dz:
                    act(row_copy(dz, 0))
                else:
                    for dx in range(1, q):
                        act(row_copy(0, dx))

        @pl.when(r >= z)
        def _():
            for dr in range(1, R):
                for tx in range(q):
                    act(col_copy(dr, tx))

    for copy in own:
        copy.wait()
    pl.semaphore_wait(barrier, (z + 1) * q * G - 1 + jnp.where(r >= z, (R - 1) * q, 0))
    moves(lambda copy: copy.start())

    for h in range(nh // LANES):
        hubcol[h * LANES:(h + 1) * LANES, :] = jnp.transpose(
            jnp.broadcast_to(ids_ref[h:h + 1, :], (LANES, LANES)))

    def hub_hits(base):
        return hubcol[...] == base + lax.broadcasted_iota(jnp.int32, (nh, LANES), 1)

    def light_lanes(t, carry):
        hit = jnp.max(jnp.where(hub_hits(t * LANES), 1, 0), axis=0, keepdims=True)
        keep[pl.ds(t, 1), :] = hit - 1
        return carry

    tiles = bc // LANES
    lax.fori_loop(0, C * tiles, light_lanes, 0)

    def keep_of(block, first=0, count=tiles):
        return jnp.concatenate([keep[pl.ds(block * tiles + first + t, 1), :] for t in range(count)], axis=1)

    part = pl.ds(pl.multiple_of(g * pc, LANES), pc)
    once = (g == 0).astype(jnp.float32)
    wide = q * pc + ng

    def wait_row(k):
        pltpu.make_async_copy(rowbuf.at[k], rowbuf.at[k], row_recv.at[k]).wait()

    def wait_hub(slot):
        pltpu.make_async_copy(hubbuf.at[slot], hubbuf.at[slot], hub_recv.at[slot]).wait()

    def wait_col(plane, tx):
        pltpu.make_async_copy(colbuf.at[plane, tx], colbuf.at[plane, tx], col_recv.at[plane, tx]).wait()

    def load_a(k):
        mask = keep_of(k)
        for w in range(bw):
            abuf[32 * w:32 * w + 32, :] = spread(rowbuf[k, w:w + 1, :] & mask, 1.0).astype(jnp.bfloat16)
        for j in range(G):
            for w in range(hw):
                lo = rows + 32 * (j * hw + w)
                abuf[lo:lo + 32, :] = spread(hubbuf[j * C + k, w:w + 1, :] & mask, 1.0).astype(jnp.bfloat16)

    def hub_rows(block, value):
        return jnp.transpose(jnp.concatenate(
            [spread(hubbuf[g * C + block, w:w + 1, :], value) for w in range(hw)], axis=0))

    def load_b(plane, weight):
        for tx in range(q):
            for w in range(wq):
                bits = colbuf[plane, tx, pl.ds(x * wq - begin(x) + w, 1), part]
                bbuf[32 * w:32 * w + 32, tx * pc:(tx + 1) * pc] = spread(bits, weight).astype(jnp.bfloat16)

        @pl.when(z == 0)
        def _():
            bbuf[:, q * pc:wide] = hub_rows(plane * q + x, 2.0).astype(jnp.bfloat16)

    masks = []

    def close(product, fresh):
        def tail(lo, total):
            wsum[lo:lo + 32, :] = total if fresh else wsum[lo:lo + 32, :] + total

        def hits(words, lo):
            found = []
            for tx in range(q):
                hit = spread(words(tx) & masks[tx], product[lo:lo + 32, tx * pc:(tx + 1) * pc])
                found += [hit[:, t * LANES:(t + 1) * LANES] for t in range(pc // LANES)]
            return functools.reduce(jnp.add, found)

        for w in range(bw):
            lo = 32 * w
            found = hits(lambda tx: rowbuf[z * q + tx, w:w + 1, part], lo)
            for t in range(ng // LANES):
                lanes = slice(t * LANES, (t + 1) * LANES)
                found += home[lo:lo + 32, lanes] * product[lo:lo + 32, q * pc + t * LANES:q * pc + (t + 1) * LANES]
            tail(lo, found)
        for j in range(G):
            for w in range(hw):
                tail(rows + 32 * (j * hw + w),
                     hits(lambda tx: hubbuf[j * C + z * q + tx, w:w + 1, part], rows + 32 * (j * hw + w)))

    load_a(c)
    bbuf[:, wide:] = jnp.broadcast_to(once, (bc, LANES)).astype(jnp.bfloat16)

    @pl.when(z > 0)
    def _():
        bbuf[:, q * pc:wide] = jnp.zeros((bc, ng), jnp.bfloat16)
        home[...] = jnp.zeros((rows, ng), jnp.float32)

    for dx in range(q):
        for dg in range(G):
            if dx or dg:
                wait_hub((g + dg) % G * C + z * q + (x + dx) % q)
        if dx:
            wait_row(z * q + (x + dx) % q)
    for tx in range(q):
        colbuf[r, tx] = rowbuf[z * q + tx, pl.ds(begin(x), size), :]
        masks.append(keep_of(z * q + tx, g * (pc // LANES), pc // LANES))

    @pl.when(r != z)
    def _():
        for tx in range(q):
            wait_col(z, tx)

    for dz in range(1, R):
        @pl.when(z + dz < R)
        def _():
            for dx in range(q):
                for dg in range(G):
                    if dx:
                        wait_hub((g + dg) % G * C + (z + dz) * q + (x + dx) % q)
                    elif dg:
                        wait_hub((g + dg) % G * C + (z + dz) * q + x)
                    else:
                        wait_hub(g * C + (z + dz) * q + x)

    @pl.when(z == 0)
    def _():
        for k in range(q):
            home[k * bc:(k + 1) * bc, :] = hub_rows(r * q + k, 1.0)

    load_b(z, 1.0)
    product = jnp.dot(abuf[...], bbuf[...], preferred_element_type=jnp.float32)
    degs[...] = product[:, wide:]
    close(product, True)

    @pl.when(jnp.logical_and(z == 0, x == 0))
    def _():
        for t in range(ng // LANES):
            degs[:rows, :] += jnp.broadcast_to(
                jnp.sum(home[:, t * LANES:(t + 1) * LANES], axis=1, keepdims=True), (rows, LANES))

    def step(dz, carry):
        plane = z + dz
        k = plane * q + x

        @pl.when(plane != r)
        def _():
            for tx in range(q):
                wait_col(plane, tx)

        wait_row(k)
        load_a(k)
        load_b(plane, 2.0)
        close(jnp.dot(abuf[...], bbuf[:, :wide], preferred_element_type=jnp.float32), False)
        return carry

    lax.fori_loop(1, R - z, step, 0)

    hub_tri = jnp.sum(wsum[rows:, :], axis=1, keepdims=True)
    hub_deg = degs[rows:, :]

    def settle(to, d):
        hits = hub_hits(r * rows + to * per)
        light = 1.0 - jnp.sum(jnp.where(hits, 1.0, 0.0), axis=0, keepdims=True)
        start = pl.multiple_of(to * per, 8)
        tri = jnp.sum(jnp.transpose(wsum[pl.ds(start, LANES), :]), axis=0, keepdims=True)
        deg = jnp.transpose(degs[pl.ds(start, LANES), :])[:1, :]
        outbox[d, 0:1, :] = light * tri + jnp.sum(jnp.where(hits, hub_tri, 0.0), axis=0, keepdims=True)
        outbox[d, 1:2, :] = light * deg + jnp.sum(jnp.where(hits, hub_deg, 0.0), axis=0, keepdims=True)

    posts = []
    for d in range(1, G * C):
        slot = (me + d) % (G * C)
        settle(slot % C, d)
        post = pltpu.make_async_remote_copy(
            src_ref=outbox.at[d], dst_ref=inbox.at[me], send_sem=msg_send.at[d], recv_sem=msg_recv.at[me],
            device_id=(r, slot % C, slot // C), device_id_type=MESH)
        post.start()
        posts.append(post)

    settle(c, 0)
    tri = outbox[0, 0:1, :]
    deg = outbox[0, 1:2, :]
    for d in range(1, G * C):
        slot = (me + d) % (G * C)
        pltpu.make_async_copy(inbox.at[slot], inbox.at[slot], msg_recv.at[slot]).wait()
        tri = tri + inbox[slot, 0:1, :]
        deg = deg + inbox[slot, 1:2, :]
    out_ref[...] = (0.5 * tri / (1.0 + deg))[:, :per]
    moves(lambda copy: copy.wait_send())
    for copy in posts:
        copy.wait_send()


def body(light_bits, hub_bits, hub_ids):
    R, C, G = lax.axis_size("rows"), lax.axis_size("cols"), lax.axis_size("hub")
    bw, bc = light_bits.shape
    hw = hub_bits.shape[0]
    nh = hub_ids.shape[0]
    rows, pc = 32 * bw, bc // G
    per = rows // C
    q = C // R
    wide = q * pc + nh // G
    _, size = piece(bw, bw // q, q)
    dma = pltpu.SemaphoreType.DMA
    hbm = pl.BlockSpec(memory_space=pltpu.HBM)
    buffers = [
        ((nh // LANES, LANES), jnp.int32),
        ((C, bw, bc), jnp.int32),
        ((R, q, size, bc), jnp.int32),
        ((G * C, hw, bc), jnp.int32),
        ((C * bc // LANES, LANES), jnp.int32),
        ((nh, LANES), jnp.int32),
        ((rows + nh, bc), jnp.bfloat16),
        ((bc, wide + LANES), jnp.bfloat16),
        ((rows, nh // G), jnp.float32),
        ((rows + nh, LANES), jnp.float32),
        ((rows + nh, LANES), jnp.float32),
        ((G * C, 2, LANES), jnp.float32),
        ((G * C, 2, LANES), jnp.float32),
        ((G * C, 1, LANES), jnp.float32),
    ]
    held = sum(math.prod(shape) * jnp.dtype(dtype).itemsize for shape, dtype in buffers)
    held += 4 * (rows + nh) * (wide + LANES)
    out = pl.pallas_call(
        functools.partial(kernel, R, C, G),
        out_shape=jax.ShapeDtypeStruct((1, per), jnp.float32),
        in_specs=[hbm, hbm, hbm],
        out_specs=pl.BlockSpec(memory_space=pltpu.VMEM),
        scratch_shapes=[pltpu.VMEM(shape, dtype) for shape, dtype in buffers] + [
            dma((3,)), dma((R, q)), dma((C,)), dma((R, q)), dma((R, q)),
            dma((R, q, G)), dma((G * C,)), dma((G * C,)), dma((G * C,)),
        ],
        compiler_params=pltpu.CompilerParams(
            collective_id=0, has_side_effects=True, vmem_limit_bytes=held + 12 * 1024 * 1024),
    )(*(pltpu.with_memory_space_constraint(x, pltpu.HBM)
        for x in (light_bits, hub_bits, hub_ids.reshape(nh // LANES, LANES))))
    return out.reshape(per)


def solution(mesh):
    return jax.shard_map(
        body,
        mesh=mesh,
        in_specs=(P("rows", "cols"), P("hub", "cols"), P()),
        out_specs=P(("rows", "cols")),
        check_vma=False,
    )
```

time: 20.5 us -> 19.6 us (0.956)
  Pallas kernels: 19.8 us -> 18.9 us
    pallas_call x1, Pallas kernels: 19.8 us -> 18.9 us  [body(): pl.pallas_call(functools.partial(kernel, R, C, G), out_shape=jax.ShapeDty...]
where the time goes in v2:
time: 19.6 us; the launch traced here: 19.4 us
  Pallas kernels  18.9 us (96%)
  local copies, waits for them, and re-layouts  0.51 us (3%)
    pallas_call x1, Pallas kernels, body(): pl.pallas_call(functools.partial(kernel, R, C, G), out_shape=jax.ShapeDty...  18.9 us
    unnamed x1, local copies, waits for them, and re-layouts  0.51 us

profile of v2, /device:TPU:0, one launch (start us, length us, event | category | flops | bytes accessed | tf_op | source)
XLA Modules:
  0.0 19.4 jit_solution(5477944060071873703)
XLA Ops:
  0.0 18.9 %shard_map.37 = f32[1,96]{1,0:T(1,128)S(1)} custom-call(s32[24,384]{1,0:T(8,128)} %light_hbm.1, s32[4,384]{1,0:T(4,128)} %hub_hbm.1, s32[1,128]{1,0:T(1,128)} %bitcast.3), custom_call_target="tpu_custom_call" | custom-call | tf_op jit(solution)/shard_map/pallas_call | solution.py:334
  18.9 0.5 %copy.5 = f32[96]{0:T(128)} copy(f32[96]{0:T(128)S(1)} %bitcast.2) | data formatting | bytes 768

commit v3 on v2

--- a/solution.py
+++ b/solution.py
@@ -9,6 +9,7 @@
 from jax.sharding import PartitionSpec as P
 
 LANES = 128
+BIT = jnp.float8_e4m3fn
 MESH = pl.DeviceIdType.MESH
 
 
@@ -28,7 +29,7 @@
 def kernel(
     R, C, G,
     light_hbm, hub_hbm, ids_hbm, out_ref,
-    ids_ref, rowbuf, colbuf, hubbuf, keep, hubcol, abuf, bbuf, home, degs, wsum, outbox, inbox, flags,
+    ids_ref, rowbuf, colbuf, hubbuf, keep, hubcol, abuf, bbuf, mask, owner, light, wsum, outbox, inbox,
     local_sem, row_send, row_recv, col_send, col_recv, hub_send, hub_recv, msg_send, msg_recv,
 ):
     r, c, g = lax.axis_index("rows"), lax.axis_index("cols"), lax.axis_index("hub")
@@ -149,61 +150,51 @@
     def wait_col(plane, tx):
         pltpu.make_async_copy(colbuf.at[plane, tx], colbuf.at[plane, tx], col_recv.at[plane, tx]).wait()
 
-    def load_a(k):
-        mask = keep_of(k)
+    def load_light(k):
+        kept = keep_of(k)
         for w in range(bw):
-            abuf[32 * w:32 * w + 32, :] = spread(rowbuf[k, w:w + 1, :] & mask, 1.0).astype(jnp.bfloat16)
+            abuf[32 * w:32 * w + 32, :] = spread(rowbuf[k, w:w + 1, :] & kept, 1.0).astype(BIT)
+
+    def load_hubs(k):
+        kept = keep_of(k)
         for j in range(G):
             for w in range(hw):
                 lo = rows + 32 * (j * hw + w)
-                abuf[lo:lo + 32, :] = spread(hubbuf[j * C + k, w:w + 1, :] & mask, 1.0).astype(jnp.bfloat16)
+                abuf[lo:lo + 32, :] = spread(hubbuf[j * C + k, w:w + 1, :] & kept, 1.0).astype(BIT)
 
     def hub_rows(block, value):
         return jnp.transpose(jnp.concatenate(
             [spread(hubbuf[g * C + block, w:w + 1, :], value) for w in range(hw)], axis=0))
+
+    def load_side(plane):
+        @pl.when(z == 0)
+        def _():
+            bbuf[:, q * pc:] = hub_rows(plane * q + x, 2.0).astype(BIT)
 
     def load_b(plane, weight):
         for tx in range(q):
             for w in range(wq):
                 bits = colbuf[plane, tx, pl.ds(x * wq - begin(x) + w, 1), part]
-                bbuf[32 * w:32 * w + 32, tx * pc:(tx + 1) * pc] = spread(bits, weight).astype(jnp.bfloat16)
-
-        @pl.when(z == 0)
-        def _():
-            bbuf[:, q * pc:wide] = hub_rows(plane * q + x, 2.0).astype(jnp.bfloat16)
-
-    masks = []
+                bbuf[32 * w:32 * w + 32, tx * pc:(tx + 1) * pc] = spread(bits, weight).astype(BIT)
 
     def close(product, fresh):
-        def tail(lo, total):
-            wsum[lo:lo + 32, :] = total if fresh else wsum[lo:lo + 32, :] + total
-
-        def hits(words, lo):
-            found = []
-            for tx in range(q):
-                hit = spread(words(tx) & masks[tx], product[lo:lo + 32, tx * pc:(tx + 1) * pc])
-                found += [hit[:, t * LANES:(t + 1) * LANES] for t in range(pc // LANES)]
-            return functools.reduce(jnp.add, found)
-
-        for w in range(bw):
-            lo = 32 * w
-            found = hits(lambda tx: rowbuf[z * q + tx, w:w + 1, part], lo)
-            for t in range(ng // LANES):
-                lanes = slice(t * LANES, (t + 1) * LANES)
-                found += home[lo:lo + 32, lanes] * product[lo:lo + 32, q * pc + t * LANES:q * pc + (t + 1) * LANES]
-            tail(lo, found)
-        for j in range(G):
-            for w in range(hw):
-                tail(rows + 32 * (j * hw + w),
-                     hits(lambda tx: hubbuf[j * C + z * q + tx, w:w + 1, part], rows + 32 * (j * hw + w)))
-
-    load_a(c)
-    bbuf[:, wide:] = jnp.broadcast_to(once, (bc, LANES)).astype(jnp.bfloat16)
+        for lo in range(0, rows + nh, 32):
+            found = functools.reduce(jnp.add, [
+                mask[lo:lo + 32, at:at + LANES] * product[lo:lo + 32, at:at + LANES]
+                for at in range(0, wide if lo < rows else q * pc, LANES)])
+            wsum[lo:lo + 32, :] = found if fresh else wsum[lo:lo + 32, :] + found
+
+    load_light(c)
+    for t in range(rows // LANES):
+        lanes = slice(t * LANES, (t + 1) * LANES)
+        hits = jnp.where(hub_hits(r * rows + t * LANES), 1.0, 0.0)
+        owner[:, lanes] = hits
+        light[:, lanes] = 1.0 - jnp.sum(hits, axis=0, keepdims=True)
 
     @pl.when(z > 0)
     def _():
-        bbuf[:, q * pc:wide] = jnp.zeros((bc, ng), jnp.bfloat16)
-        home[...] = jnp.zeros((rows, ng), jnp.float32)
+        bbuf[:, q * pc:] = jnp.zeros((bc, ng), BIT)
+        mask[:rows, q * pc:] = jnp.zeros((rows, ng), jnp.float32)
 
     for dx in range(q):
         for dg in range(G):
@@ -211,9 +202,42 @@
                 wait_hub((g + dg) % G * C + z * q + (x + dx) % q)
         if dx:
             wait_row(z * q + (x + dx) % q)
+    load_hubs(c)
     for tx in range(q):
         colbuf[r, tx] = rowbuf[z * q + tx, pl.ds(begin(x), size), :]
-        masks.append(keep_of(z * q + tx, g * (pc // LANES), pc // LANES))
+        kept = keep_of(z * q + tx, g * (pc // LANES), pc // LANES)
+        lanes = slice(tx * pc, (tx + 1) * pc)
+        for w in range(bw):
+            mask[32 * w:32 * w + 32, lanes] = spread(rowbuf[z * q + tx, w:w + 1, part] & kept, 1.0)
+        for j in range(G):
+            for w in range(hw):
+                lo = rows + 32 * (j * hw + w)
+                mask[lo:lo + 32, lanes] = spread(hubbuf[j * C + z * q + tx, w:w + 1, part] & kept, 1.0)
+
+    def over_lanes(row):
+        return functools.reduce(jnp.add, [row[:, t * LANES:(t + 1) * LANES] for t in range(tiles)])
+
+    kept = keep_of(c)
+    hub_deg = jnp.sum(jnp.concatenate([
+        over_lanes(spread(hubbuf[j * C + c, w:w + 1, :] & kept, 1.0)) for j in range(G) for w in range(hw)],
+        axis=0), axis=1, keepdims=True) * once
+
+    def turn(matrix):
+        ones = jnp.ones((8, matrix.shape[1]), matrix.dtype)
+        return lax.dot_general(
+            ones, matrix, (((1,), (1,)), ((), ())), preferred_element_type=jnp.float32)[:1, :]
+
+    def owned(row, column):
+        return light[...] * row + jnp.sum(owner[...] * column, axis=0, keepdims=True)
+
+    deg_row = owned(turn(abuf[:rows, :]) * once, hub_deg)
+
+    def post(row, value):
+        for slot in range(G * C):
+            to = slot % C
+            outbox[slot, row:row + 1, :per] = value[:, to * per:(to + 1) * per]
+
+    post(1, deg_row)
 
     @pl.when(r != z)
     def _():
@@ -225,28 +249,24 @@
         def _():
             for dx in range(q):
                 for dg in range(G):
-                    if dx:
-                        wait_hub((g + dg) % G * C + (z + dz) * q + (x + dx) % q)
-                    elif dg:
-                        wait_hub((g + dg) % G * C + (z + dz) * q + x)
-                    else:
-                        wait_hub(g * C + (z + dz) * q + x)
+                    wait_hub((g + dg) % G * C + (z + dz) * q + (x + dx) % q)
 
     @pl.when(z == 0)
     def _():
         for k in range(q):
-            home[k * bc:(k + 1) * bc, :] = hub_rows(r * q + k, 1.0)
-
-    load_b(z, 1.0)
-    product = jnp.dot(abuf[...], bbuf[...], preferred_element_type=jnp.float32)
-    degs[...] = product[:, wide:]
-    close(product, True)
+            mask[k * bc:(k + 1) * bc, q * pc:] = hub_rows(r * q + k, 1.0)
 
     @pl.when(jnp.logical_and(z == 0, x == 0))
     def _():
-        for t in range(ng // LANES):
-            degs[:rows, :] += jnp.broadcast_to(
-                jnp.sum(home[:, t * LANES:(t + 1) * LANES], axis=1, keepdims=True), (rows, LANES))
+        extra = light[...] * jnp.concatenate([
+            jnp.sum(functools.reduce(jnp.add, [
+                spread(hubbuf[g * C + r * q + k, w:w + 1, :], 1.0) for w in range(hw)]), axis=0, keepdims=True)
+            for k in range(q)], axis=1)
+        post(1, deg_row + extra)
+
+    load_side(z)
+    load_b(z, 1.0)
+    close(jnp.dot(abuf[...], bbuf[...], preferred_element_type=jnp.float32), True)
 
     def step(dz, carry):
         plane = z + dz
@@ -257,39 +277,39 @@
             for tx in range(q):
                 wait_col(plane, tx)
 
+        load_side(plane)
         wait_row(k)
-        load_a(k)
         load_b(plane, 2.0)
-        close(jnp.dot(abuf[...], bbuf[:, :wide], preferred_element_type=jnp.float32), False)
+        load_hubs(k)
+        load_light(k)
+        close(jnp.dot(abuf[...], bbuf[...], preferred_element_type=jnp.float32), False)
         return carry
 
     lax.fori_loop(1, R - z, step, 0)
 
     hub_tri = jnp.sum(wsum[rows:, :], axis=1, keepdims=True)
-    hub_deg = degs[rows:, :]
-
-    def settle(to, d):
-        hits = hub_hits(r * rows + to * per)
-        light = 1.0 - jnp.sum(jnp.where(hits, 1.0, 0.0), axis=0, keepdims=True)
-        start = pl.multiple_of(to * per, 8)
-        tri = jnp.sum(jnp.transpose(wsum[pl.ds(start, LANES), :]), axis=0, keepdims=True)
-        deg = jnp.transpose(degs[pl.ds(start, LANES), :])[:1, :]
-        outbox[d, 0:1, :] = light * tri + jnp.sum(jnp.where(hits, hub_tri, 0.0), axis=0, keepdims=True)
-        outbox[d, 1:2, :] = light * deg + jnp.sum(jnp.where(hits, hub_deg, 0.0), axis=0, keepdims=True)
-
-    posts = []
-    for d in range(1, G * C):
-        slot = (me + d) % (G * C)
-        settle(slot % C, d)
-        post = pltpu.make_async_remote_copy(
-            src_ref=outbox.at[d], dst_ref=inbox.at[me], send_sem=msg_send.at[d], recv_sem=msg_recv.at[me],
+    rest = wsum[:rows, :]
+    tri_row = jnp.zeros((1, rows), jnp.float32)
+    for _ in range(3):
+        upper = rest.astype(jnp.bfloat16)
+        tri_row = tri_row + turn(upper)
+        rest = rest - upper.astype(jnp.float32)
+    post(0, owned(tri_row, hub_tri))
+
+    def message(slot):
+        return pltpu.make_async_remote_copy(
+            src_ref=outbox.at[slot], dst_ref=inbox.at[me], send_sem=msg_send.at[slot], recv_sem=msg_recv.at[me],
             device_id=(r, slot % C, slot // C), device_id_type=MESH)
-        post.start()
-        posts.append(post)
-
-    settle(c, 0)
-    tri = outbox[0, 0:1, :]
-    deg = outbox[0, 1:2, :]
+
+    def messages(act):
+        for slot in range(G * C):
+            @pl.when(slot != me)
+            def _():
+                act(message(slot))
+
+    messages(lambda copy: copy.start())
+    tri = outbox[me, 0:1, :]
+    deg = outbox[me, 1:2, :]
     for d in range(1, G * C):
         slot = (me + d) % (G * C)
         pltpu.make_async_copy(inbox.at[slot], inbox.at[slot], msg_recv.at[slot]).wait()
@@ -297,8 +317,7 @@
         deg = deg + inbox[slot, 1:2, :]
     out_ref[...] = (0.5 * tri / (1.0 + deg))[:, :per]
     moves(lambda copy: copy.wait_send())
-    for copy in posts:
-        copy.wait_send()
+    messages(lambda copy: copy.wait_send())
 
 
 def body(light_bits, hub_bits, hub_ids):
@@ -320,17 +339,17 @@
         ((G * C, hw, bc), jnp.int32),
         ((C * bc // LANES, LANES), jnp.int32),
         ((nh, LANES), jnp.int32),
-        ((rows + nh, bc), jnp.bfloat16),
-        ((bc, wide + LANES), jnp.bfloat16),
-        ((rows, nh // G), jnp.float32),
-        ((rows + nh, LANES), jnp.float32),
+        ((rows + nh, bc), BIT),
+        ((bc, wide), BIT),
+        ((rows + nh, wide), jnp.float32),
+        ((nh, rows), jnp.float32),
+        ((1, rows), jnp.float32),
         ((rows + nh, LANES), jnp.float32),
         ((G * C, 2, LANES), jnp.float32),
         ((G * C, 2, LANES), jnp.float32),
-        ((G * C, 1, LANES), jnp.float32),
     ]
     held = sum(math.prod(shape) * jnp.dtype(dtype).itemsize for shape, dtype in buffers)
-    held += 4 * (rows + nh) * (wide + LANES)
+    held += 4 * (rows + nh) * wide
     out = pl.pallas_call(
         functools.partial(kernel, R, C, G),
         out_shape=jax.ShapeDtypeStruct((1, per), jnp.float32),

time: 19.6 us -> 16.6 us (0.85)
  Pallas kernels: 18.9 us -> 15.9 us
    pallas_call x1, Pallas kernels: 18.9 us -> 15.9 us  [body(): pl.pallas_call(functools.partial(kernel, R, C, G), out_shape=jax.ShapeDty...]
where the time goes in v3:
time: 16.6 us; the launch traced here: 16.4 us
  Pallas kernels  15.9 us (96%)
  local copies, waits for them, and re-layouts  0.51 us (3%)
    pallas_call x1, Pallas kernels, body(): pl.pallas_call(functools.partial(kernel, R, C, G), out_shape=jax.ShapeDty...  15.9 us
    unnamed x1, local copies, waits for them, and re-layouts  0.51 us

profile of v3, /device:TPU:0, one launch (start us, length us, event | category | flops | bytes accessed | tf_op | source)
XLA Modules:
  0.0 16.4 jit_solution(10596032109897115043)
XLA Ops:
  0.0 15.9 %shard_map.37 = f32[1,96]{1,0:T(1,128)S(1)} custom-call(s32[24,384]{1,0:T(8,128)} %light_hbm.1, s32[4,384]{1,0:T(4,128)} %hub_hbm.1, s32[1,128]{1,0:T(1,128)} %bitcast.3), custom_call_target="tpu_custom_call" | custom-call | tf_op jit(solution)/shard_map/pallas_call | solution.py:353
  15.9 0.5 %copy.5 = f32[96]{0:T(128)} copy(f32[96]{0:T(128)S(1)} %bitcast.2) | data formatting | bytes 768

commit v4 on v3

v4 whole, which is shorter than its diff:
```python
import functools
import math

import jax
import jax.numpy as jnp
from jax import lax
from jax.experimental import pallas as pl
from jax.experimental.pallas import tpu as pltpu
from jax.sharding import PartitionSpec as P

LANES = 128
BIT = jnp.float8_e4m3fn
MESH = pl.DeviceIdType.MESH


def spread(row, value, other=0.0):
    masks = jnp.left_shift(jnp.int32(1), lax.broadcasted_iota(jnp.int32, (32, row.shape[1]), 0))
    return jnp.where((jnp.broadcast_to(row, masks.shape) & masks) != 0, value, other)


def pieces(wq, x):
    cuts = [x * wq] + [t for t in range(8, (x + 1) * wq, 8) if t > x * wq] + [(x + 1) * wq]
    parts = []
    for lo, hi in zip(cuts, cuts[1:]):
        if parts and lo % 8 == 0 and hi % 8 == 0 and parts[-1][0] % 8 == 0 and sum(parts[-1]) == lo:
            parts[-1] = (parts[-1][0], hi - parts[-1][0])
        else:
            parts.append((lo, hi - lo))
    return parts


def shape_of(wq, q):
    size = max(-(-(x + 1) * wq // 8) * 8 - x * wq // 8 * 8 for x in range(q))
    return size, max(len(pieces(wq, x)) for x in range(q))


def kernel(
    R, C, G,
    light_hbm, hub_hbm, ids_hbm, out_ref,
    ids_ref, rowbuf, colbuf, hubbuf, keep, hubcol, abuf, bbuf, home, side, owner, light, product, wsum, outbox, inbox,
    local_sem, row_send, row_recv, col_send, col_recv, hub_send, hub_recv, msg_send, msg_recv, seen,
):
    r, c, g = lax.axis_index("rows"), lax.axis_index("cols"), lax.axis_index("hub")
    _, bw, bc = rowbuf.shape
    hw = hubbuf.shape[1]
    pc = bc // G
    q = C // R
    z, x = c // q, c % q
    rows = 32 * bw
    wq = bw // q
    ng = 32 * hw
    nh = ng * G
    per = rows // C
    me = g * C + c

    own = [
        pltpu.make_async_copy(light_hbm, rowbuf.at[c], local_sem.at[0]),
        pltpu.make_async_copy(hub_hbm, hubbuf.at[me], local_sem.at[1]),
        pltpu.make_async_copy(ids_hbm, ids_ref, local_sem.at[2]),
    ]
    for copy in own:
        copy.start()

    def at(plane, dx, dg=0):
        return (r, plane * q + (x + dx) % q, (g + dg) % G)

    barrier = pltpu.get_barrier_semaphore()

    def greet(device):
        pl.semaphore_signal(barrier, inc=1, device_id=device, device_id_type=MESH)

    for dz in range(R):
        @pl.when(z + dz < R)
        def _():
            for dx in range(q):
                for dg in range(G):
                    if dz or dx or dg:
                        greet(at(z + dz, dx, dg))
    for dr in range(1, R):
        @pl.when((r + dr) % R >= z)
        def _():
            for dx in range(q):
                greet(((r + dr) % R, z * q + dx, g))

    def row_copy(dz, dx):
        return pltpu.make_async_remote_copy(
            src_ref=rowbuf.at[c], dst_ref=rowbuf.at[c], send_sem=row_send.at[dz, dx], recv_sem=row_recv.at[c],
            device_id=at(z - dz, dx), device_id_type=MESH)

    def hub_copy(dz, dx, dg):
        return pltpu.make_async_remote_copy(
            src_ref=hubbuf.at[me], dst_ref=hubbuf.at[me], send_sem=hub_send.at[dz, dx, dg],
            recv_sem=hub_recv.at[me], device_id=at(z - dz, dx, dg), device_id_type=MESH)

    def homing(dx):
        return pltpu.make_async_remote_copy(
            src_ref=hubbuf.at[me], dst_ref=hubbuf.at[me], send_sem=hub_send.at[R, dx, 0],
            recv_sem=hub_recv.at[me], device_id=at(0, dx), device_id_type=MESH)

    def col_copies(to, tx):
        base = tx * wq // 8 * 8
        return [
            pltpu.make_async_remote_copy(
                src_ref=rowbuf.at[c, pl.ds(lo, size), :], dst_ref=colbuf.at[r, x, pl.ds(lo - base, size), :],
                send_sem=col_send.at[to, tx, n], recv_sem=col_recv.at[r, x, n],
                device_id=(to, z * q + tx, g), device_id_type=MESH)
            for n, (lo, size) in enumerate(pieces(wq, tx))]

    def moves(act):
        @pl.when(jnp.logical_and(z == r, z > 0))
        def _():
            for dx in range(1, q):
                act(homing(dx))

        for dz in range(R - 1, -1, -1):
            @pl.when(z >= dz)
            def _():
                for dx in range(q if dz == 0 else 1):
                    for dg in range(G):
                        if dz or dx or dg:
                            act(hub_copy(dz, dx, dg))
                if dz:
                    act(row_copy(dz, 0))
                else:
                    for dx in range(1, q):
                        act(row_copy(0, dx))

        @pl.when(r >= z)
        def _():
            for to in range(R):
                @pl.when(r != to)
                def _():
                    for tx in range(q):
                        for copy in col_copies(to, tx):
                            act(copy)

    for copy in own:
        copy.wait()
    pl.semaphore_wait(barrier, (z + 1) * q * G - 1 + jnp.where(r >= z, (R - 1) * q, 0))
    moves(lambda copy: copy.start())
    for dz in range(1, R):
        for dx in range(1, q):
            for dg in range(G):
                homed = jnp.logical_and(z == r, z == dz) if dg == 0 else False

                @pl.when(jnp.logical_and(z >= dz, jnp.logical_not(homed)))
                def _():
                    pl.semaphore_signal(seen, inc=1, device_id=at(z - dz, dx, dg), device_id_type=MESH)

    for h in range(nh // LANES):
        hubcol[h * LANES:(h + 1) * LANES, :] = jnp.transpose(
            jnp.broadcast_to(ids_ref[h:h + 1, :], (LANES, LANES)))

    def hub_hits(base):
        return hubcol[...] == base + lax.broadcasted_iota(jnp.int32, (nh, LANES), 1)

    def light_lanes(t, carry):
        hit = jnp.max(jnp.where(hub_hits(t * LANES), 1, 0), axis=0, keepdims=True)
        keep[pl.ds(t, 1), :] = hit - 1
        return carry

    tiles = bc // LANES
    lax.fori_loop(0, C * tiles, light_lanes, 0)

    def keep_of(block, first=0, count=tiles):
        return jnp.concatenate([keep[pl.ds(block * tiles + first + t, 1), :] for t in range(count)], axis=1)

    part = pl.ds(pl.multiple_of(g * pc, LANES), pc)

    def wait_row(k):
        pltpu.make_async_copy(rowbuf.at[k], rowbuf.at[k], row_recv.at[k]).wait()

    def wait_hub(slot):
        pltpu.make_async_copy(hubbuf.at[slot], hubbuf.at[slot], hub_recv.at[slot]).wait()

    def wait_cols(plane):
        for mine in range(q):
            @pl.when(jnp.logical_and(plane != r, x == mine))
            def _():
                for tx in range(q):
                    for n, (lo, size) in enumerate(pieces(wq, mine)):
                        ref = colbuf.at[plane, tx, pl.ds(lo - mine * wq // 8 * 8, size), :]
                        pltpu.make_async_copy(ref, ref, col_recv.at[plane, tx, n]).wait()

    def part_keep(tx):
        return keep_of(z * q + tx, g * (pc // LANES), pc // LANES)

    def lanes_of(tx):
        return pl.ds(pl.multiple_of(tx * pc, LANES), pc)

    def load_light(tx):
        kept = part_keep(tx)
        for w in range(bw):
            abuf[32 * w:32 * w + 32, lanes_of(tx)] = spread(
                rowbuf[z * q + tx, w:w + 1, part] & kept, 1.0).astype(BIT)

    def load_hubs(tx):
        kept = part_keep(tx)
        for j in range(G):
            for w in range(hw):
                lo = rows + 32 * (j * hw + w)
                abuf[lo:lo + 32, lanes_of(tx)] = spread(
                    hubbuf[j * C + z * q + tx, w:w + 1, part] & kept, 1.0).astype(BIT)

    def load_b(plane, base):
        first = x * wq - x * wq // 8 * 8
        weight = jnp.where(plane == z, 1.0, 2.0)
        for tx in range(q):
            for w in range(wq):
                bits = colbuf[plane, tx, pl.ds(first + w, 1), part]
                bbuf[base + 32 * w:base + 32 * w + 32, tx * pc:(tx + 1) * pc] = spread(bits, weight).astype(BIT)

        for w in range(hw):
            side[32 * w:32 * w + 32, base:base + bc] = spread(
                hubbuf[g * C + plane * q + x, w:w + 1, :], 2.0).astype(BIT)

    def load_home():
        @pl.when(r > 0)
        def _():
            for dx in range(q):
                wait_hub(g * C + r * q + (x + dx) % q)

        for k in range(q):
            home[k * bc:(k + 1) * bc, :] = jnp.transpose(jnp.concatenate(
                [spread(hubbuf[g * C + r * q + k, w:w + 1, :], 1.0) for w in range(hw)], axis=0)).astype(BIT)

    def multiply(planes):
        deep = len(planes) * bc
        for n, plane in enumerate(planes):
            load_b(plane, n * bc)
        all_rows = lax.dot_general(
            abuf[...], bbuf[:deep, :], (((1,), (1,)), ((), ())), preferred_element_type=jnp.float32)
        product[:rows, :deep] = all_rows[:rows, :] + jnp.dot(
            home[...], side[:, :deep], preferred_element_type=jnp.float32)
        product[rows:, :deep] = all_rows[rows:, :]

    def over_lanes(row):
        return functools.reduce(jnp.add, [row[:, t:t + LANES] for t in range(0, row.shape[1], LANES)])

    def close(plane, base):
        k = plane * q + x
        kept = keep_of(k)

        def add(word, lo):
            found = over_lanes(spread(word & kept, product[lo:lo + 32, base:base + bc]))
            wsum[lo:lo + 32, :] += found

        for w in range(bw):
            add(rowbuf[k, w:w + 1, :], 32 * w)
        for j in range(G):
            for w in range(hw):
                add(hubbuf[j * C + k, w:w + 1, :], rows + 32 * (j * hw + w))

    wsum[...] = jnp.zeros_like(wsum)
    load_light(x)
    for t in range(rows // LANES):
        lanes = slice(t * LANES, (t + 1) * LANES)
        hits = jnp.where(hub_hits(r * rows + t * LANES), 1.0, 0.0)
        owner[:, lanes] = hits
        light[:, lanes] = 1.0 - jnp.sum(hits, axis=0, keepdims=True)

    for dg in range(1, G):
        wait_hub((g + dg) % G * C + c)
    load_hubs(x)

    kept = part_keep(x)
    hub_deg = jnp.sum(jnp.concatenate([
        over_lanes(spread(hubbuf[j * C + c, w:w + 1, part] & kept, 1.0)) for j in range(G) for w in range(hw)],
        axis=0), axis=1, keepdims=True)

    def turn(matrix):
        ones = jnp.ones((8, matrix.shape[1]), matrix.dtype)
        return lax.dot_general(
            ones, matrix, (((1,), (1,)), ((), ())), preferred_element_type=jnp.float32)[:1, :]

    def owned(row, column):
        return light[...] * row + jnp.sum(owner[...] * column, axis=0, keepdims=True)

    def post(row, value):
        for slot in range(G * C):
            to = slot % C
            outbox[slot, row:row + 1, :per] = value[:, to * per:(to + 1) * per]

    deg_row = owned(turn(abuf[:rows, lanes_of(x)]), hub_deg)
    post(1, deg_row)

    for dx in range(1, q):
        other = (x + dx) % q
        for dg in range(G):
            wait_hub((g + dg) % G * C + z * q + other)
        load_hubs(other)
    for dx in range(1, q):
        other = (x + dx) % q
        wait_row(z * q + other)
        load_light(other)

    base = x * wq // 8 * 8
    for tx in range(q):
        colbuf[r, tx] = rowbuf[z * q + tx, pl.ds(pl.multiple_of(base, 8), colbuf.shape[2]), :]

    @pl.when(z > 0)
    def _():
        home[...] = jnp.zeros((rows, ng), BIT)

    @pl.when(z == 0)
    def _():
        load_home()

        @pl.when(x == 0)
        def _():
            extra = light[...] * jnp.concatenate([
                jnp.sum(functools.reduce(jnp.add, [
                    spread(hubbuf[g * C + r * q + k, w:w + 1, :], 1.0) for w in range(hw)]), axis=0, keepdims=True)
                for k in range(q)], axis=1)
            post(1, deg_row + extra)

    def wait_hubs(plane):
        for dg in range(G):
            @pl.when(jnp.logical_and(plane > z, jnp.logical_not(jnp.logical_and(z == 0, plane == r)))
                     if dg == 0 else plane > z)
            def _():
                wait_hub((g + dg) % G * C + plane * q + x)

    def steps(planes):
        for plane in planes:
            wait_cols(plane)
            wait_hubs(plane)
        multiply(planes)
        for n, plane in enumerate(planes):
            pl.when(plane > z)(functools.partial(wait_row, plane * q + x))
            close(plane, n * bc)

    odd = (R - z) % 2

    @pl.when(odd == 1)
    def _():
        steps([z])

    def pair(n, carry):
        first = z + odd + 2 * n
        steps([first, first + 1])
        return carry

    lax.fori_loop(0, (R - z) // 2, pair, 0)

    hub_tri = jnp.sum(wsum[rows:, :], axis=1, keepdims=True)
    rest = wsum[:rows, :]
    tri_row = jnp.zeros((1, rows), jnp.float32)
    for _ in range(3):
        upper = rest.astype(jnp.bfloat16)
        tri_row = tri_row + turn(upper)
        rest = rest - upper.astype(jnp.float32)
    post(0, owned(tri_row, hub_tri))

    def message(slot):
        return pltpu.make_async_remote_copy(
            src_ref=outbox.at[slot], dst_ref=inbox.at[me], send_sem=msg_send.at[slot], recv_sem=msg_recv.at[me],
            device_id=(r, slot % C, slot // C), device_id_type=MESH)

    def messages(act):
        for slot in range(G * C):
            @pl.when(slot != me)
            def _():
                act(message(slot))

    @pl.when(z < R - 1)
    def _():
        pl.semaphore_wait(seen, (R - 1 - z) * (q - 1) * G - jnp.where(jnp.logical_and(z == 0, r > 0), q - 1, 0))

    messages(lambda copy: copy.start())
    tri = outbox[me, 0:1, :]
    deg = outbox[me, 1:2, :]
    for d in range(1, G * C):
        slot = (me + d) % (G * C)
        pltpu.make_async_copy(inbox.at[slot], inbox.at[slot], msg_recv.at[slot]).wait()
        tri = tri + inbox[slot, 0:1, :]
        deg = deg + inbox[slot, 1:2, :]
    out_ref[...] = (0.5 * tri / (1.0 + deg))[:, :per]
    moves(lambda copy: copy.wait_send())
    messages(lambda copy: copy.wait_send())


def body(light_bits, hub_bits, hub_ids):
    R, C, G = lax.axis_size("rows"), lax.axis_size("cols"), lax.axis_size("hub")
    bw, bc = light_bits.shape
    hw = hub_bits.shape[0]
    nh = hub_ids.shape[0]
    rows, pc = 32 * bw, bc // G
    per = rows // C
    q = C // R
    size, count = shape_of(bw // q, q)
    dma = pltpu.SemaphoreType.DMA
    hbm = pl.BlockSpec(memory_space=pltpu.HBM)
    buffers = [
        ((nh // LANES, LANES), jnp.int32),
        ((C, bw, bc), jnp.int32),
        ((R, q, size, bc), jnp.int32),
        ((G * C, hw, bc), jnp.int32),
        ((C * bc // LANES, LANES), jnp.int32),
        ((nh, LANES), jnp.int32),
        ((rows + nh, q * pc), BIT),
        ((2 * bc, q * pc), BIT),
        ((rows, nh // G), BIT),
        ((nh // G, 2 * bc), BIT),
        ((nh, rows), jnp.float32),
        ((1, rows), jnp.float32),
        ((rows + nh, 2 * bc), jnp.float32),
        ((rows + nh, LANES), jnp.float32),
        ((G * C, 2, LANES), jnp.float32),
        ((G * C, 2, LANES), jnp.float32),
    ]
    held = sum(math.prod(shape) * jnp.dtype(dtype).itemsize for shape, dtype in buffers)
    held += 8 * (rows + nh) * bc
    out = pl.pallas_call(
        functools.partial(kernel, R, C, G),
        out_shape=jax.ShapeDtypeStruct((1, per), jnp.float32),
        in_specs=[hbm, hbm, hbm],
        out_specs=pl.BlockSpec(memory_space=pltpu.VMEM),
        scratch_shapes=[pltpu.VMEM(shape, dtype) for shape, dtype in buffers] + [
            dma((3,)), dma((R, q)), dma((C,)), dma((R, q, count)), dma((R, q, count)),
            dma((R + 1, q, G)), dma((G * C,)), dma((G * C,)), dma((G * C,)), pltpu.SemaphoreType.REGULAR,
        ],
        compiler_params=pltpu.CompilerParams(
            collective_id=0, has_side_effects=True, vmem_limit_bytes=held + 12 * 1024 * 1024),
    )(*(pltpu.with_memory_space_constraint(x, pltpu.HBM)
        for x in (light_bits, hub_bits, hub_ids.reshape(nh // LANES, LANES))))
    return out.reshape(per)


def solution(mesh):
    return jax.shard_map(
        body,
        mesh=mesh,
        in_specs=(P("rows", "cols"), P("hub", "cols"), P()),
        out_specs=P(("rows", "cols")),
        check_vma=False,
    )
```

time: 16.6 us -> 15.4 us (0.928)
  Pallas kernels: 15.9 us -> 14.7 us
    pallas_call x1, Pallas kernels: 15.9 us -> 14.7 us  [body(): pl.pallas_call(functools.partial(kernel, R, C, G), out_shape=jax.ShapeDty...]
where the time goes in v4:
time: 15.4 us; the launch traced here: 15.2 us
  Pallas kernels  14.7 us (95%)
  local copies, waits for them, and re-layouts  0.51 us (3%)
    pallas_call x1, Pallas kernels, body(): pl.pallas_call(functools.partial(kernel, R, C, G), out_shape=jax.ShapeDty...  14.7 us
    unnamed x1, local copies, waits for them, and re-layouts  0.51 us

profile of v4, /device:TPU:0, one launch (start us, length us, event | category | flops | bytes accessed | tf_op | source)
XLA Modules:
  0.0 15.2 jit_solution(1920783343116660221)
XLA Ops:
  0.0 14.7 %shard_map.37 = f32[1,96]{1,0:T(1,128)S(1)} custom-call(s32[24,384]{1,0:T(8,128)} %light_hbm.1, s32[4,384]{1,0:T(4,128)} %hub_hbm.1, s32[1,128]{1,0:T(1,128)} %bitcast.3), custom_call_target="tpu_custom_call" | custom-call | tf_op jit(solution)/shard_map/pallas_call | solution.py:414
  14.7 0.5 %copy.5 = f32[96]{0:T(128)} copy(f32[96]{0:T(128)S(1)} %bitcast.2) | data formatting | bytes 768

commit v5 on v4

--- a/solution.py
+++ b/solution.py
@@ -37,7 +37,7 @@
 def kernel(
     R, C, G,
     light_hbm, hub_hbm, ids_hbm, out_ref,
-    ids_ref, rowbuf, colbuf, hubbuf, keep, hubcol, abuf, bbuf, home, side, owner, light, product, wsum, outbox, inbox,
+    ids_ref, rowbuf, colbuf, hubbuf, keep, hubcol, abuf, bbuf, owner, light, product, wsum, outbox, inbox,
     local_sem, row_send, row_recv, col_send, col_recv, hub_send, hub_recv, msg_send, msg_recv, seen,
 ):
     r, c, g = lax.axis_index("rows"), lax.axis_index("cols"), lax.axis_index("hub")
@@ -106,38 +106,52 @@
                 device_id=(to, z * q + tx, g), device_id_type=MESH)
             for n, (lo, size) in enumerate(pieces(wq, tx))]
 
-    def moves(act):
-        @pl.when(jnp.logical_and(z == r, z > 0))
-        def _():
-            for dx in range(1, q):
-                act(homing(dx))
-
-        for dz in range(R - 1, -1, -1):
-            @pl.when(z >= dz)
-            def _():
-                for dx in range(q if dz == 0 else 1):
-                    for dg in range(G):
-                        if dz or dx or dg:
-                            act(hub_copy(dz, dx, dg))
-                if dz:
-                    act(row_copy(dz, 0))
-                else:
-                    for dx in range(1, q):
-                        act(row_copy(0, dx))
-
+    def send_cols(act, targets):
         @pl.when(r >= z)
         def _():
-            for to in range(R):
+            for to in targets:
                 @pl.when(r != to)
                 def _():
                     for tx in range(q):
                         for copy in col_copies(to, tx):
                             act(copy)
 
+    def send_near(act):
+        @pl.when(jnp.logical_and(z == r, z > 0))
+        def _():
+            for dx in range(1, q):
+                act(homing(dx))
+
+        send_cols(act, range(1))
+        for dx in range(q):
+            for dg in range(G):
+                if dx or dg:
+                    act(hub_copy(0, dx, dg))
+        for dx in range(1, q):
+            act(row_copy(0, dx))
+
+    def send_far(act):
+        for dz in [1] + list(range(R - 1, 1, -1)):
+            @pl.when(z >= dz)
+            def _():
+                for dg in range(G):
+                    act(hub_copy(dz, 0, dg))
+                act(row_copy(dz, 0))
+
+    def moves(act):
+        send_near(act)
+        send_far(act)
+        send_cols(act, range(1, R))
+
     for copy in own:
         copy.wait()
     pl.semaphore_wait(barrier, (z + 1) * q * G - 1 + jnp.where(r >= z, (R - 1) * q, 0))
-    moves(lambda copy: copy.start())
+    def start(copy):
+        copy.start()
+
+    send_near(start)
+    send_far(start)
+    send_cols(start, range(1, R))
     for dz in range(1, R):
         for dx in range(1, q):
             for dg in range(G):
@@ -202,17 +216,19 @@
                 abuf[lo:lo + 32, lanes_of(tx)] = spread(
                     hubbuf[j * C + z * q + tx, w:w + 1, part] & kept, 1.0).astype(BIT)
 
-    def load_b(plane, base):
+    def load_b(plane, base, hubs):
         first = x * wq - x * wq // 8 * 8
         weight = jnp.where(plane == z, 1.0, 2.0)
         for tx in range(q):
             for w in range(wq):
                 bits = colbuf[plane, tx, pl.ds(first + w, 1), part]
                 bbuf[base + 32 * w:base + 32 * w + 32, tx * pc:(tx + 1) * pc] = spread(bits, weight).astype(BIT)
-
-        for w in range(hw):
-            side[32 * w:32 * w + 32, base:base + bc] = spread(
-                hubbuf[g * C + plane * q + x, w:w + 1, :], 2.0).astype(BIT)
+        if hubs:
+            bbuf[base:base + bc, q * pc:] = hub_rows(plane * q + x, 2.0)
+
+    def hub_rows(block, value):
+        return jnp.transpose(jnp.concatenate(
+            [spread(hubbuf[g * C + block, w:w + 1, :], value) for w in range(hw)], axis=0)).astype(BIT)
 
     def load_home():
         @pl.when(r > 0)
@@ -221,18 +237,17 @@
                 wait_hub(g * C + r * q + (x + dx) % q)
 
         for k in range(q):
-            home[k * bc:(k + 1) * bc, :] = jnp.transpose(jnp.concatenate(
-                [spread(hubbuf[g * C + r * q + k, w:w + 1, :], 1.0) for w in range(hw)], axis=0)).astype(BIT)
-
-    def multiply(planes):
+            abuf[k * bc:(k + 1) * bc, q * pc:] = hub_rows(r * q + k, 1.0)
+        abuf[rows:, q * pc:] = jnp.zeros((nh, ng), BIT)
+
+    def multiply(planes, hubs):
         deep = len(planes) * bc
         for n, plane in enumerate(planes):
-            load_b(plane, n * bc)
-        all_rows = lax.dot_general(
-            abuf[...], bbuf[:deep, :], (((1,), (1,)), ((), ())), preferred_element_type=jnp.float32)
-        product[:rows, :deep] = all_rows[:rows, :] + jnp.dot(
-            home[...], side[:, :deep], preferred_element_type=jnp.float32)
-        product[rows:, :deep] = all_rows[rows:, :]
+            load_b(plane, n * bc, hubs)
+        wide = q * pc + (ng if hubs else 0)
+        product[:, :deep] = lax.dot_general(
+            abuf[:, :wide], bbuf[:deep, :wide], (((1,), (1,)), ((), ())), preferred_element_type=jnp.float32)
+        close(planes[0], 0)
 
     def over_lanes(row):
         return functools.reduce(jnp.add, [row[:, t:t + LANES] for t in range(0, row.shape[1], LANES)])
@@ -298,10 +313,6 @@
     for tx in range(q):
         colbuf[r, tx] = rowbuf[z * q + tx, pl.ds(pl.multiple_of(base, 8), colbuf.shape[2]), :]
 
-    @pl.when(z > 0)
-    def _():
-        home[...] = jnp.zeros((rows, ng), BIT)
-
     @pl.when(z == 0)
     def _():
         load_home()
@@ -321,24 +332,26 @@
             def _():
                 wait_hub((g + dg) % G * C + plane * q + x)
 
-    def steps(planes):
+    def meet_row(plane):
+        pl.when(plane > z)(functools.partial(wait_row, plane * q + x))
+
+    odd = (R - z) % 2
+
+    @pl.when(odd == 1)
+    def _():
+        wait_cols(z)
+        multiply([z], R % 2 == 1)
+
+    def pair(n, carry):
+        planes = [z + odd + 2 * n, z + odd + 2 * n + 1]
         for plane in planes:
             wait_cols(plane)
             wait_hubs(plane)
-        multiply(planes)
-        for n, plane in enumerate(planes):
-            pl.when(plane > z)(functools.partial(wait_row, plane * q + x))
-            close(plane, n * bc)
-
-    odd = (R - z) % 2
-
-    @pl.when(odd == 1)
-    def _():
-        steps([z])
-
-    def pair(n, carry):
-        first = z + odd + 2 * n
-        steps([first, first + 1])
+        meet_row(planes[0])
+        pl.when(z == 0)(functools.partial(multiply, planes, True))
+        pl.when(z > 0)(functools.partial(multiply, planes, False))
+        wait_row(planes[1] * q + x)
+        close(planes[1], bc)
         return carry
 
     lax.fori_loop(0, (R - z) // 2, pair, 0)
@@ -346,7 +359,8 @@
     hub_tri = jnp.sum(wsum[rows:, :], axis=1, keepdims=True)
     rest = wsum[:rows, :]
     tri_row = jnp.zeros((1, rows), jnp.float32)
-    for _ in range(3):
+    largest = 2 * (q * pc + ng) * R * (bc // LANES)
+    for _ in range(-(-largest.bit_length() // 8)):
         upper = rest.astype(jnp.bfloat16)
         tri_row = tri_row + turn(upper)
         rest = rest - upper.astype(jnp.float32)
@@ -398,10 +412,8 @@
         ((G * C, hw, bc), jnp.int32),
         ((C * bc // LANES, LANES), jnp.int32),
         ((nh, LANES), jnp.int32),
-        ((rows + nh, q * pc), BIT),
-        ((2 * bc, q * pc), BIT),
-        ((rows, nh // G), BIT),
-        ((nh // G, 2 * bc), BIT),
+        ((rows + nh, q * pc + nh // G), BIT),
+        ((2 * bc, q * pc + nh // G), BIT),
         ((nh, rows), jnp.float32),
         ((1, rows), jnp.float32),
         ((rows + nh, 2 * bc), jnp.float32),

time: 15.4 us -> 14.7 us (0.955)
  Pallas kernels: 14.7 us -> 14 us
    pallas_call x1, Pallas kernels: 14.7 us -> 14 us  [body(): pl.pallas_call(functools.partial(kernel, R, C, G), out_shape=jax.ShapeDty...]
where the time goes in v5:
time: 14.7 us; the launch traced here: 14.5 us
  Pallas kernels  14 us (95%)
  local copies, waits for them, and re-layouts  0.51 us (3%)
    pallas_call x1, Pallas kernels, body(): pl.pallas_call(functools.partial(kernel, R, C, G), out_shape=jax.ShapeDty...  14 us
    unnamed x1, local copies, waits for them, and re-layouts  0.51 us

profile of v5, /device:TPU:0, one launch (start us, length us, event | category | flops | bytes accessed | tf_op | source)
XLA Modules:
  0.0 14.5 jit_solution(15539152890885353728)
XLA Ops:
  0.0 14.0 %shard_map.37 = f32[1,96]{1,0:T(1,128)S(1)} custom-call(s32[24,384]{1,0:T(8,128)} %light_hbm.1, s32[4,384]{1,0:T(4,128)} %hub_hbm.1, s32[1,128]{1,0:T(1,128)} %bitcast.3), custom_call_target="tpu_custom_call" | custom-call | tf_op jit(solution)/shard_map/pallas_call | solution.py:426
  14.0 0.5 %copy.5 = f32[96]{0:T(128)} copy(f32[96]{0:T(128)S(1)} %bitcast.2) | data formatting | bytes 768

commit v6 on v5

--- a/solution.py
+++ b/solution.py
@@ -51,6 +51,8 @@
     ng = 32 * hw
     nh = ng * G
     per = rows // C
+    lead = -(-per // LANES) * LANES
+    front = nh + lead
     me = g * C + c
 
     own = [
@@ -205,14 +207,14 @@
     def load_light(tx):
         kept = part_keep(tx)
         for w in range(bw):
-            abuf[32 * w:32 * w + 32, lanes_of(tx)] = spread(
+            abuf[nh + 32 * w:nh + 32 * w + 32, lanes_of(tx)] = spread(
                 rowbuf[z * q + tx, w:w + 1, part] & kept, 1.0).astype(BIT)
 
     def load_hubs(tx):
         kept = part_keep(tx)
         for j in range(G):
             for w in range(hw):
-                lo = rows + 32 * (j * hw + w)
+                lo = 32 * (j * hw + w)
                 abuf[lo:lo + 32, lanes_of(tx)] = spread(
                     hubbuf[j * C + z * q + tx, w:w + 1, part] & kept, 1.0).astype(BIT)
 
@@ -237,34 +239,28 @@
                 wait_hub(g * C + r * q + (x + dx) % q)
 
         for k in range(q):
-            abuf[k * bc:(k + 1) * bc, q * pc:] = hub_rows(r * q + k, 1.0)
-        abuf[rows:, q * pc:] = jnp.zeros((nh, ng), BIT)
-
-    def multiply(planes, hubs):
-        deep = len(planes) * bc
+            abuf[nh + k * bc:nh + (k + 1) * bc, q * pc:] = hub_rows(r * q + k, 1.0)
+
+    def multiply(planes, base, hubs):
+        wide = q * pc + (ng if hubs else 0)
         for n, plane in enumerate(planes):
             load_b(plane, n * bc, hubs)
-        wide = q * pc + (ng if hubs else 0)
-        product[:, :deep] = lax.dot_general(
+        deep = len(planes) * bc
+        product[:, base:base + deep] = lax.dot_general(
             abuf[:, :wide], bbuf[:deep, :wide], (((1,), (1,)), ((), ())), preferred_element_type=jnp.float32)
-        close(planes[0], 0)
 
     def over_lanes(row):
         return functools.reduce(jnp.add, [row[:, t:t + LANES] for t in range(0, row.shape[1], LANES)])
 
-    def close(plane, base):
+    def close(plane, base, start, stop):
         k = plane * q + x
         kept = keep_of(k)
-
-        def add(word, lo):
-            found = over_lanes(spread(word & kept, product[lo:lo + 32, base:base + bc]))
-            wsum[lo:lo + 32, :] += found
-
-        for w in range(bw):
-            add(rowbuf[k, w:w + 1, :], 32 * w)
-        for j in range(G):
-            for w in range(hw):
-                add(hubbuf[j * C + k, w:w + 1, :], rows + 32 * (j * hw + w))
+        words = [(j, w) for j in range(G) for w in range(hw)] + [(G, w) for w in range(bw)]
+        for n in range(start // 32, stop // 32):
+            j, w = words[n]
+            bits = (hubbuf[j * C + k, w:w + 1, :] if j < G else rowbuf[k, w:w + 1, :]) & kept
+            at = slice(32 * n, 32 * n + 32)
+            wsum[at, :] += over_lanes(spread(bits, product[at, base:base + bc]))
 
     wsum[...] = jnp.zeros_like(wsum)
     load_light(x)
@@ -288,15 +284,18 @@
         return lax.dot_general(
             ones, matrix, (((1,), (1,)), ((), ())), preferred_element_type=jnp.float32)[:1, :]
 
-    def owned(row, column):
-        return light[...] * row + jnp.sum(owner[...] * column, axis=0, keepdims=True)
-
-    def post(row, value):
+    def owned(row, column, start=0):
+        lanes = slice(start, start + row.shape[1])
+        return light[:, lanes] * row + jnp.sum(owner[:, lanes] * column, axis=0, keepdims=True)
+
+    def post(row, value, owners=range(C)):
         for slot in range(G * C):
             to = slot % C
+            if to not in owners:
+                continue
             outbox[slot, row:row + 1, :per] = value[:, to * per:(to + 1) * per]
 
-    deg_row = owned(turn(abuf[:rows, lanes_of(x)]), hub_deg)
+    deg_row = owned(turn(abuf[nh:, lanes_of(x)]), hub_deg)
     post(1, deg_row)
 
     for dx in range(1, q):
@@ -315,6 +314,7 @@
 
     @pl.when(z == 0)
     def _():
+        abuf[:nh, q * pc:] = jnp.zeros((nh, ng), BIT)
         load_home()
 
         @pl.when(x == 0)
@@ -336,11 +336,20 @@
         pl.when(plane > z)(functools.partial(wait_row, plane * q + x))
 
     odd = (R - z) % 2
+    last = R - 1
 
     @pl.when(odd == 1)
     def _():
         wait_cols(z)
-        multiply([z], R % 2 == 1)
+
+        @pl.when(z < last)
+        def _():
+            multiply([z], bc, R % 2 == 1)
+            close(z, bc, 0, nh + rows)
+
+        @pl.when(z == last)
+        def _():
+            multiply([z], bc, R == 1)
 
     def pair(n, carry):
         planes = [z + odd + 2 * n, z + odd + 2 * n + 1]
@@ -348,40 +357,60 @@
             wait_cols(plane)
             wait_hubs(plane)
         meet_row(planes[0])
-        pl.when(z == 0)(functools.partial(multiply, planes, True))
-        pl.when(z > 0)(functools.partial(multiply, planes, False))
+        for hubs, mine in [(True, z == 0), (False, z > 0)]:
+            @pl.when(mine)
+            def _():
+                multiply(planes, 0, hubs)
+                close(planes[0], 0, 0, nh + rows)
+
         wait_row(planes[1] * q + x)
-        close(planes[1], bc)
+
+        @pl.when(planes[1] < last)
+        def _():
+            close(planes[1], bc, 0, nh + rows)
+
         return carry
 
     lax.fori_loop(0, (R - z) // 2, pair, 0)
-
-    hub_tri = jnp.sum(wsum[rows:, :], axis=1, keepdims=True)
-    rest = wsum[:rows, :]
-    tri_row = jnp.zeros((1, rows), jnp.float32)
+    close(last, bc, 0, front)
     largest = 2 * (q * pc + ng) * R * (bc // LANES)
-    for _ in range(-(-largest.bit_length() // 8)):
-        upper = rest.astype(jnp.bfloat16)
-        tri_row = tri_row + turn(upper)
-        rest = rest - upper.astype(jnp.float32)
-    post(0, owned(tri_row, hub_tri))
+
+    def row_sums(start, stop):
+        rest = wsum[start:stop, :]
+        row = jnp.zeros((1, stop - start), jnp.float32)
+        for _ in range(-(-largest.bit_length() // 8)):
+            upper = rest.astype(jnp.bfloat16)
+            row = row + turn(upper)
+            rest = rest - upper.astype(jnp.float32)
+        return row
 
     def message(slot):
         return pltpu.make_async_remote_copy(
             src_ref=outbox.at[slot], dst_ref=inbox.at[me], send_sem=msg_send.at[slot], recv_sem=msg_recv.at[me],
             device_id=(r, slot % C, slot // C), device_id_type=MESH)
 
-    def messages(act):
+    def messages(act, owners):
         for slot in range(G * C):
-            @pl.when(slot != me)
-            def _():
-                act(message(slot))
+            if slot % C in owners:
+                @pl.when(slot != me)
+                def _():
+                    act(message(slot))
+
+    hub_tri = jnp.sum(wsum[:nh, :], axis=1, keepdims=True)
+    lead_row = owned(row_sums(nh, front), hub_tri)
+    for slot in range(0, G * C, C):
+        outbox[slot, 0:1, :per] = lead_row[:, :per]
+    messages(start, range(1))
+
+    close(last, bc, front, nh + rows)
+    later = range(1, C)
+    post(0, jnp.concatenate([lead_row, owned(row_sums(front, nh + rows), hub_tri, lead)], axis=1), later)
 
     @pl.when(z < R - 1)
     def _():
         pl.semaphore_wait(seen, (R - 1 - z) * (q - 1) * G - jnp.where(jnp.logical_and(z == 0, r > 0), q - 1, 0))
 
-    messages(lambda copy: copy.start())
+    messages(start, later)
     tri = outbox[me, 0:1, :]
     deg = outbox[me, 1:2, :]
     for d in range(1, G * C):
@@ -391,7 +420,7 @@
         deg = deg + inbox[slot, 1:2, :]
     out_ref[...] = (0.5 * tri / (1.0 + deg))[:, :per]
     moves(lambda copy: copy.wait_send())
-    messages(lambda copy: copy.wait_send())
+    messages(lambda copy: copy.wait_send(), range(C))
 
 
 def body(light_bits, hub_bits, hub_ids):

time: 14.7 us -> 14.4 us (0.980)
  Pallas kernels: 14 us -> 13.7 us
    pallas_call x1, Pallas kernels: 14 us -> 13.7 us  [body(): pl.pallas_call(functools.partial(kernel, R, C, G), out_shape=jax.ShapeDty...]
where the time goes in v6:
time: 14.4 us; the launch traced here: 14.2 us
  Pallas kernels  13.7 us (95%)
  local copies, waits for them, and re-layouts  0.51 us (4%)
    pallas_call x1, Pallas kernels, body(): pl.pallas_call(functools.partial(kernel, R, C, G), out_shape=jax.ShapeDty...  13.7 us
    unnamed x1, local copies, waits for them, and re-layouts  0.51 us

profile of v6, /device:TPU:0, one launch (start us, length us, event | category | flops | bytes accessed | tf_op | source)
XLA Modules:
  0.0 14.2 jit_solution(13232224071778121904)
XLA Ops:
  0.0 13.7 %shard_map.37 = f32[1,96]{1,0:T(1,128)S(1)} custom-call(s32[24,384]{1,0:T(8,128)} %light_hbm.1, s32[4,384]{1,0:T(4,128)} %hub_hbm.1, s32[1,128]{1,0:T(1,128)} %bitcast.3), custom_call_target="tpu_custom_call" | custom-call | tf_op jit(solution)/shard_map/pallas_call | solution.py:455
  13.7 0.5 %copy.5 = f32[96]{0:T(128)} copy(f32[96]{0:T(128)S(1)} %bitcast.2) | data formatting | bytes 768

commit v7 on v6

--- a/solution.py
+++ b/solution.py
@@ -29,9 +29,8 @@
     return parts
 
 
-def shape_of(wq, q):
-    size = max(-(-(x + 1) * wq // 8) * 8 - x * wq // 8 * 8 for x in range(q))
-    return size, max(len(pieces(wq, x)) for x in range(q))
+def size_of(wq, q):
+    return max(-(-(x + 1) * wq // 8) * 8 - x * wq // 8 * 8 for x in range(q))
 
 
 def kernel(
@@ -86,27 +85,27 @@
 
     def row_copy(dz, dx):
         return pltpu.make_async_remote_copy(
-            src_ref=rowbuf.at[c], dst_ref=rowbuf.at[c], send_sem=row_send.at[dz, dx], recv_sem=row_recv.at[c],
+            src_ref=rowbuf.at[c], dst_ref=rowbuf.at[c], send_sem=row_send.at[0], recv_sem=row_recv.at[dz],
             device_id=at(z - dz, dx), device_id_type=MESH)
 
     def hub_copy(dz, dx, dg):
         return pltpu.make_async_remote_copy(
-            src_ref=hubbuf.at[me], dst_ref=hubbuf.at[me], send_sem=hub_send.at[dz, dx, dg],
-            recv_sem=hub_recv.at[me], device_id=at(z - dz, dx, dg), device_id_type=MESH)
+            src_ref=hubbuf.at[me], dst_ref=hubbuf.at[me], send_sem=hub_send.at[0],
+            recv_sem=hub_recv.at[2 + dz if dz else min(dx, 1)], device_id=at(z - dz, dx, dg), device_id_type=MESH)
 
     def homing(dx):
         return pltpu.make_async_remote_copy(
-            src_ref=hubbuf.at[me], dst_ref=hubbuf.at[me], send_sem=hub_send.at[R, dx, 0],
-            recv_sem=hub_recv.at[me], device_id=at(0, dx), device_id_type=MESH)
+            src_ref=hubbuf.at[me], dst_ref=hubbuf.at[me], send_sem=hub_send.at[0],
+            recv_sem=hub_recv.at[2], device_id=at(0, dx), device_id_type=MESH)
 
     def col_copies(to, tx):
         base = tx * wq // 8 * 8
         return [
             pltpu.make_async_remote_copy(
                 src_ref=rowbuf.at[c, pl.ds(lo, size), :], dst_ref=colbuf.at[r, x, pl.ds(lo - base, size), :],
-                send_sem=col_send.at[to, tx, n], recv_sem=col_recv.at[r, x, n],
+                send_sem=col_send.at[0], recv_sem=col_recv.at[r],
                 device_id=(to, z * q + tx, g), device_id_type=MESH)
-            for n, (lo, size) in enumerate(pieces(wq, tx))]
+            for lo, size in pieces(wq, tx)]
 
     def send_cols(act, targets):
         @pl.when(r >= z)
@@ -140,10 +139,24 @@
                     act(hub_copy(dz, 0, dg))
                 act(row_copy(dz, 0))
 
-    def moves(act):
-        send_near(act)
-        send_far(act)
-        send_cols(act, range(1, R))
+    def drain(buffer, count, sem):
+        if count:
+            ref = buffer.at[pl.ds(0, count)]
+            pltpu.make_async_copy(ref, ref, sem).wait()
+
+    def wait_sends():
+        for plane in range(R):
+            @pl.when(z == plane)
+            def _():
+                drain(rowbuf, plane + q - 1, row_send.at[0])
+                homed = r == z if plane else False
+                for more in (0, 1) if plane else (0,):
+                    @pl.when(homed if more else jnp.logical_not(homed))
+                    def _():
+                        drain(hubbuf, plane * G + q * G - 1 + more * (q - 1), hub_send.at[0])
+
+        pl.when(r >= z)(lambda: drain(rowbuf, R - 1, col_send.at[0]))
+        drain(outbox, G * C - 1, msg_send.at[0])
 
     for copy in own:
         copy.wait()
@@ -183,20 +196,8 @@
 
     part = pl.ds(pl.multiple_of(g * pc, LANES), pc)
 
-    def wait_row(k):
-        pltpu.make_async_copy(rowbuf.at[k], rowbuf.at[k], row_recv.at[k]).wait()
-
-    def wait_hub(slot):
-        pltpu.make_async_copy(hubbuf.at[slot], hubbuf.at[slot], hub_recv.at[slot]).wait()
-
     def wait_cols(plane):
-        for mine in range(q):
-            @pl.when(jnp.logical_and(plane != r, x == mine))
-            def _():
-                for tx in range(q):
-                    for n, (lo, size) in enumerate(pieces(wq, mine)):
-                        ref = colbuf.at[plane, tx, pl.ds(lo - mine * wq // 8 * 8, size), :]
-                        pltpu.make_async_copy(ref, ref, col_recv.at[plane, tx, n]).wait()
+        pl.when(plane != r)(lambda: drain(rowbuf, 1, col_recv.at[plane]))
 
     def part_keep(tx):
         return keep_of(z * q + tx, g * (pc // LANES), pc // LANES)
@@ -235,8 +236,8 @@
     def load_home():
         @pl.when(r > 0)
         def _():
-            for dx in range(q):
-                wait_hub(g * C + r * q + (x + dx) % q)
+            drain(hubbuf, G, hub_recv.at[2 + r])
+            drain(hubbuf, q - 1, hub_recv.at[2])
 
         for k in range(q):
             abuf[nh + k * bc:nh + (k + 1) * bc, q * pc:] = hub_rows(r * q + k, 1.0)
@@ -270,8 +271,7 @@
         owner[:, lanes] = hits
         light[:, lanes] = 1.0 - jnp.sum(hits, axis=0, keepdims=True)
 
-    for dg in range(1, G):
-        wait_hub((g + dg) % G * C + c)
+    drain(hubbuf, G - 1, hub_recv.at[0])
     load_hubs(x)
 
     kept = part_keep(x)
@@ -298,14 +298,13 @@
     deg_row = owned(turn(abuf[nh:, lanes_of(x)]), hub_deg)
     post(1, deg_row)
 
+    drain(hubbuf, (q - 1) * G, hub_recv.at[1])
     for dx in range(1, q):
         other = (x + dx) % q
-        for dg in range(G):
-            wait_hub((g + dg) % G * C + z * q + other)
         load_hubs(other)
+    drain(rowbuf, q - 1, row_recv.at[0])
     for dx in range(1, q):
         other = (x + dx) % q
-        wait_row(z * q + other)
         load_light(other)
 
     base = x * wq // 8 * 8
@@ -326,14 +325,17 @@
             post(1, deg_row + extra)
 
     def wait_hubs(plane):
-        for dg in range(G):
-            @pl.when(jnp.logical_and(plane > z, jnp.logical_not(jnp.logical_and(z == 0, plane == r)))
-                     if dg == 0 else plane > z)
-            def _():
-                wait_hub((g + dg) % G * C + plane * q + x)
+        homed = jnp.logical_and(z == 0, plane == r)
+
+        @pl.when(jnp.logical_and(plane > z, jnp.logical_not(homed)))
+        def _():
+            drain(hubbuf, G, hub_recv.at[2 + plane - z])
+
+    def wait_row(plane):
+        drain(rowbuf, 1, row_recv.at[plane - z])
 
     def meet_row(plane):
-        pl.when(plane > z)(functools.partial(wait_row, plane * q + x))
+        pl.when(plane > z)(functools.partial(wait_row, plane))
 
     odd = (R - z) % 2
     last = R - 1
@@ -363,7 +365,7 @@
                 multiply(planes, 0, hubs)
                 close(planes[0], 0, 0, nh + rows)
 
-        wait_row(planes[1] * q + x)
+        wait_row(planes[1])
 
         @pl.when(planes[1] < last)
         def _():
@@ -386,7 +388,7 @@
 
     def message(slot):
         return pltpu.make_async_remote_copy(
-            src_ref=outbox.at[slot], dst_ref=inbox.at[me], send_sem=msg_send.at[slot], recv_sem=msg_recv.at[me],
+            src_ref=outbox.at[slot], dst_ref=inbox.at[me], send_sem=msg_send.at[0], recv_sem=msg_recv.at[0],
             device_id=(r, slot % C, slot // C), device_id_type=MESH)
 
     def messages(act, owners):
@@ -411,16 +413,15 @@
         pl.semaphore_wait(seen, (R - 1 - z) * (q - 1) * G - jnp.where(jnp.logical_and(z == 0, r > 0), q - 1, 0))
 
     messages(start, later)
+    wait_sends()
+    drain(inbox, G * C - 1, msg_recv.at[0])
     tri = outbox[me, 0:1, :]
     deg = outbox[me, 1:2, :]
     for d in range(1, G * C):
         slot = (me + d) % (G * C)
-        pltpu.make_async_copy(inbox.at[slot], inbox.at[slot], msg_recv.at[slot]).wait()
         tri = tri + inbox[slot, 0:1, :]
         deg = deg + inbox[slot, 1:2, :]
     out_ref[...] = (0.5 * tri / (1.0 + deg))[:, :per]
-    moves(lambda copy: copy.wait_send())
-    messages(lambda copy: copy.wait_send(), range(C))
 
 
 def body(light_bits, hub_bits, hub_ids):
@@ -431,7 +432,7 @@
     rows, pc = 32 * bw, bc // G
     per = rows // C
     q = C // R
-    size, count = shape_of(bw // q, q)
+    size = size_of(bw // q, q)
     dma = pltpu.SemaphoreType.DMA
     hbm = pl.BlockSpec(memory_space=pltpu.HBM)
     buffers = [
@@ -458,8 +459,8 @@
         in_specs=[hbm, hbm, hbm],
         out_specs=pl.BlockSpec(memory_space=pltpu.VMEM),
         scratch_shapes=[pltpu.VMEM(shape, dtype) for shape, dtype in buffers] + [
-            dma((3,)), dma((R, q)), dma((C,)), dma((R, q, count)), dma((R, q, count)),
-            dma((R + 1, q, G)), dma((G * C,)), dma((G * C,)), dma((G * C,)), pltpu.SemaphoreType.REGULAR,
+            dma((3,)), dma((1,)), dma((R,)), dma((1,)), dma((R,)),
+            dma((1,)), dma((R + 2,)), dma((1,)), dma((1,)), pltpu.SemaphoreType.REGULAR,
         ],
         compiler_params=pltpu.CompilerParams(
             collective_id=0, has_side_effects=True, vmem_limit_bytes=held + 12 * 1024 * 1024),

time: 14.4 us -> 13.8 us (0.958)
  Pallas kernels: 13.7 us -> 13.1 us
    pallas_call x1, Pallas kernels: 13.7 us -> 13.1 us  [body(): pl.pallas_call(functools.partial(kernel, R, C, G), out_shape=jax.ShapeDty...]
where the time goes in v7:
time: 13.8 us; the launch traced here: 13.6 us
  Pallas kernels  13.1 us (95%)
  local copies, waits for them, and re-layouts  0.51 us (4%)
    pallas_call x1, Pallas kernels, body(): pl.pallas_call(functools.partial(kernel, R, C, G), out_shape=jax.ShapeDty...  13.1 us
    unnamed x1, local copies, waits for them, and re-layouts  0.51 us

profile of v7, /device:TPU:0, one launch (start us, length us, event | category | flops | bytes accessed | tf_op | source)
XLA Modules:
  0.0 13.6 jit_solution(15544734768781378416)
XLA Ops:
  0.0 13.1 %shard_map.37 = f32[1,96]{1,0:T(1,128)S(1)} custom-call(s32[24,384]{1,0:T(8,128)} %light_hbm.1, s32[4,384]{1,0:T(4,128)} %hub_hbm.1, s32[1,128]{1,0:T(1,128)} %bitcast.3), custom_call_target="tpu_custom_call" | custom-call | tf_op jit(solution)/shard_map/pallas_call | solution.py:456
  13.1 0.5 %copy.5 = f32[96]{0:T(128)} copy(f32[96]{0:T(128)S(1)} %bitcast.2) | data formatting | bytes 768

commit v8 on v7

--- a/solution.py
+++ b/solution.py
@@ -91,12 +91,12 @@
     def hub_copy(dz, dx, dg):
         return pltpu.make_async_remote_copy(
             src_ref=hubbuf.at[me], dst_ref=hubbuf.at[me], send_sem=hub_send.at[0],
-            recv_sem=hub_recv.at[2 + dz if dz else min(dx, 1)], device_id=at(z - dz, dx, dg), device_id_type=MESH)
+            recv_sem=hub_recv.at[1 + dz if dz else 0 if dx else R + 1], device_id=at(z - dz, dx, dg), device_id_type=MESH)
 
     def homing(dx):
         return pltpu.make_async_remote_copy(
             src_ref=hubbuf.at[me], dst_ref=hubbuf.at[me], send_sem=hub_send.at[0],
-            recv_sem=hub_recv.at[2], device_id=at(0, dx), device_id_type=MESH)
+            recv_sem=hub_recv.at[1], device_id=at(0, dx), device_id_type=MESH)
 
     def col_copies(to, tx):
         base = tx * wq // 8 * 8
@@ -236,8 +236,8 @@
     def load_home():
         @pl.when(r > 0)
         def _():
-            drain(hubbuf, G, hub_recv.at[2 + r])
-            drain(hubbuf, q - 1, hub_recv.at[2])
+            drain(hubbuf, G, hub_recv.at[1 + r])
+            drain(hubbuf, q - 1, hub_recv.at[1])
 
         for k in range(q):
             abuf[nh + k * bc:nh + (k + 1) * bc, q * pc:] = hub_rows(r * q + k, 1.0)
@@ -271,7 +271,8 @@
         owner[:, lanes] = hits
         light[:, lanes] = 1.0 - jnp.sum(hits, axis=0, keepdims=True)
 
-    drain(hubbuf, G - 1, hub_recv.at[0])
+    if G > 1:
+        drain(hubbuf, G - 1, hub_recv.at[R + 1])
     load_hubs(x)
 
     kept = part_keep(x)
@@ -298,7 +299,7 @@
     deg_row = owned(turn(abuf[nh:, lanes_of(x)]), hub_deg)
     post(1, deg_row)
 
-    drain(hubbuf, (q - 1) * G, hub_recv.at[1])
+    drain(hubbuf, (q - 1) * G, hub_recv.at[0])
     for dx in range(1, q):
         other = (x + dx) % q
         load_hubs(other)
@@ -329,7 +330,7 @@
 
         @pl.when(jnp.logical_and(plane > z, jnp.logical_not(homed)))
         def _():
-            drain(hubbuf, G, hub_recv.at[2 + plane - z])
+            drain(hubbuf, G, hub_recv.at[1 + plane - z])
 
     def wait_row(plane):
         drain(rowbuf, 1, row_recv.at[plane - z])
@@ -359,22 +360,29 @@
             wait_cols(plane)
             wait_hubs(plane)
         meet_row(planes[0])
+        more = planes[1] < last
+
+        @pl.when(more)
+        def _():
+            wait_row(planes[1])
+
         for hubs, mine in [(True, z == 0), (False, z > 0)]:
-            @pl.when(mine)
-            def _():
-                multiply(planes, 0, hubs)
-                close(planes[0], 0, 0, nh + rows)
-
-        wait_row(planes[1])
-
-        @pl.when(planes[1] < last)
-        def _():
-            close(planes[1], bc, 0, nh + rows)
+            for both in [True, False] if R > (3 if hubs else 5) else [False]:
+                @pl.when(jnp.logical_and(mine, more if both else jnp.logical_not(more)))
+                def _():
+                    multiply(planes, 0, hubs)
+                    close(planes[0], 0, 0, nh + rows)
+                    if both:
+                        close(planes[1], bc, 0, nh + rows)
+
+        @pl.when(jnp.logical_not(more))
+        def _():
+            wait_row(planes[1])
 
         return carry
 
     lax.fori_loop(0, (R - z) // 2, pair, 0)
-    close(last, bc, 0, front)
+    pl.when(c == 0)(lambda: close(last, bc, 0, front))
     largest = 2 * (q * pc + ng) * R * (bc // LANES)
 
     def row_sums(start, stop):
@@ -392,21 +400,31 @@
             device_id=(r, slot % C, slot // C), device_id_type=MESH)
 
     def messages(act, owners):
-        for slot in range(G * C):
+        for slot in reversed(range(G * C)):
             if slot % C in owners:
                 @pl.when(slot != me)
                 def _():
                     act(message(slot))
 
+    @pl.when(c > 0)
+    def _():
+        close(last, bc, 0, front)
+        hub_tri = jnp.sum(wsum[:nh, :], axis=1, keepdims=True)
+        lead_row = owned(row_sums(nh, front), hub_tri)
+        for slot in range(0, G * C, C):
+            outbox[slot, 0:1, :per] = lead_row[:, :per]
+        messages(start, range(1))
+
+    close(last, bc, front, nh + rows)
     hub_tri = jnp.sum(wsum[:nh, :], axis=1, keepdims=True)
-    lead_row = owned(row_sums(nh, front), hub_tri)
-    for slot in range(0, G * C, C):
-        outbox[slot, 0:1, :per] = lead_row[:, :per]
-    messages(start, range(1))
-
-    close(last, bc, front, nh + rows)
+    tri_row = owned(row_sums(nh, nh + rows), hub_tri)
     later = range(1, C)
-    post(0, jnp.concatenate([lead_row, owned(row_sums(front, nh + rows), hub_tri, lead)], axis=1), later)
+    post(0, tri_row, later)
+
+    @pl.when(c == 0)
+    def _():
+        post(0, tri_row, range(1))
+        messages(start, range(1))
 
     @pl.when(z < R - 1)
     def _():
@@ -460,7 +478,7 @@
         out_specs=pl.BlockSpec(memory_space=pltpu.VMEM),
         scratch_shapes=[pltpu.VMEM(shape, dtype) for shape, dtype in buffers] + [
             dma((3,)), dma((1,)), dma((R,)), dma((1,)), dma((R,)),
-            dma((1,)), dma((R + 2,)), dma((1,)), dma((1,)), pltpu.SemaphoreType.REGULAR,
+            dma((1,)), dma((R + 1 + (G > 1),)), dma((1,)), dma((1,)), pltpu.SemaphoreType.REGULAR,
         ],
         compiler_params=pltpu.CompilerParams(
             collective_id=0, has_side_effects=True, vmem_limit_bytes=held + 12 * 1024 * 1024),

time: 13.8 us -> 13.8 us (level)
  no operation moved by 1% of the time
where the time goes in v8:
time: 13.8 us; the launch traced here: 13.6 us
  Pallas kernels  13.1 us (95%)
  local copies, waits for them, and re-layouts  0.51 us (4%)
    pallas_call x1, Pallas kernels, body(): pl.pallas_call(functools.partial(kernel, R, C, G), out_shape=jax.ShapeDty...  13.1 us
    unnamed x1, local copies, waits for them, and re-layouts  0.51 us

profile of v8, /device:TPU:0, one launch (start us, length us, event | category | flops | bytes accessed | tf_op | source)
XLA Modules:
  0.0 13.6 jit_solution(11732657829101263048)
XLA Ops:
  0.0 13.1 %shard_map.37 = f32[1,96]{1,0:T(1,128)S(1)} custom-call(s32[24,384]{1,0:T(8,128)} %light_hbm.1, s32[4,384]{1,0:T(4,128)} %hub_hbm.1, s32[1,128]{1,0:T(1,128)} %bitcast.3), custom_call_target="tpu_custom_call" | custom-call | tf_op jit(solution)/shard_map/pallas_call | solution.py:474
  13.1 0.5 %copy.5 = f32[96]{0:T(128)} copy(f32[96]{0:T(128)S(1)} %bitcast.2) | data formatting | bytes 768
